TPU v7x, 32 devices: a whole 2x2x4 slice. The times are simulated.
32 devices in a mesh: gx: 2 (over y), gy: 4 (over x, core), gz: 4 (over z).
Axes of the slice: x: 2, y: 2, z: 4, core: 2. Of those that a mesh axis runs over, the one named last changes fastest.
Arguments:
- right_side: float32 [16, 256, 512], P('gx', 'gy', 'gz'), may hold values from -4 to 4
- start: float32 [16, 256, 512], P('gx', 'gy', 'gz'), may hold values from -6 to 6
Outputs:
- solution: float32 [16, 256, 512], P('gx', 'gy', 'gz')
All inputs are finite; a program needn't handle non-finite values.
Results may differ from a plain program's by a relative error of at most 0.0003.
Values sent between devices are 32-bit elements; how exact they have to be, the bound alone decides.
A program may use at most 128 MiB of HBM per device.

v0:
```python
import functools

import jax
import jax.numpy as jnp
from jax import lax
from jax.experimental import pallas as pl
from jax.experimental.pallas import tpu as pltpu
from jax.sharding import PartitionSpec as P

MESH = pl.DeviceIdType.MESH
SIXTH = 1.0 / 6.0
PAD = 8
TOP = 16
DOWN0 = 5
SIDE0 = 4
SIDE1 = 6
RHS1 = 5
CSWEEPS = 8
CHUNK0 = 2
CHUNK1 = 4


def dot(a, b):
    return jnp.dot(a, b, precision=lax.Precision.HIGHEST, preferred_element_type=jnp.float32)


def iota(shape, axis):
    return lax.broadcasted_iota(jnp.int32, shape, axis)


def beside(v, edge):
    rows, lanes = v.shape
    up = pltpu.roll(v, 1, axis=0) + pltpu.roll(v, rows - 1, axis=0)
    low = pltpu.roll(v, 1, axis=1)
    high = pltpu.roll(v, lanes - 1, axis=1)
    if edge:
        lane = iota(v.shape, 1)
        low = jnp.where(lane == 0, 0.0, low)
        high = jnp.where(lane == lanes - 1, 0.0, high)
    return up + (low + high)


def update(v_ref, b_ref, code, first, last, origin, colour, factor, edge=False, chunk=4):
    def some(start, size):
        planes = [v_ref[start - 1 + k] for k in range(size + 2)]
        sides = [beside(planes[k + 1], edge) for k in range(size)]
        fresh = []
        for k in range(size):
            total = (planes[k] + planes[k + 2]) + sides[k]
            want = lax.rem(start + (k + origin + colour), 2)
            value = (factor * b_ref[start + k] + total) * SIXTH
            fresh.append(jnp.where(code[...] == want, value, planes[k + 1]))
        for k in range(size):
            v_ref[start + k] = fresh[k]

    if isinstance(first, int) and last - first <= chunk:
        some(first, last - first)
        return

    def body(c, carry):
        some(jnp.minimum(first + c * chunk, last - chunk), chunk)
        return carry

    lax.fori_loop(0, (last - first + chunk - 1) // chunk, body, 0)


def residual(v_ref, b_ref, i, factor, edge=False):
    v = v_ref[i]
    total = (v_ref[i - 1] + v_ref[i + 1]) + beside(v, edge)
    return b_ref[i] - (6.0 * v - total) * (1.0 / factor)


def turned(tiles, shift, edge_lane):
    moved = [pltpu.roll(tile, shift, axis=1) for tile in tiles]
    if len(moved) == 1:
        return moved
    lane = iota(tiles[0].shape, 1)
    return [jnp.where(lane == edge_lane, moved[1], moved[0]), jnp.where(lane == edge_lane, moved[0], moved[1])]


def fine_update(v_ref, b_ref, code, first, last, origin, colour, factor, chunk):
    tiles, rows = v_ref.shape[1], v_ref.shape[2] - 2 * PAD

    def some(start, size):
        planes = [[v_ref[start - 1 + k, g, PAD:PAD + rows] for g in range(tiles)] for k in range(size + 2)]
        fresh = []
        for k in range(1, size + 1):
            i = start + (k - 1)
            low = turned(planes[k], 1, 0)
            high = turned(planes[k], 127, 127)
            want = lax.rem(start + (k - 1 + origin + colour), 2)
            for g in range(tiles):
                total = v_ref[i, g, PAD - 1:PAD - 1 + rows] + v_ref[i, g, PAD + 1:PAD + 1 + rows]
                total = (total + (planes[k - 1][g] + planes[k + 1][g])) + (low[g] + high[g])
                value = (factor * b_ref[i, g, PAD:PAD + rows] + total) * SIXTH
                fresh.append((i, g, jnp.where(code[g] == want, value, planes[k][g])))
        for i, g, value in fresh:
            v_ref[i, g, PAD:PAD + rows] = value

    def body(c, carry):
        some(jnp.minimum(first + c * chunk, last - chunk), chunk)
        return carry

    lax.fori_loop(0, (last - first + chunk - 1) // chunk, body, 0)


def fine_residual(v_ref, b_ref, i, rows, factor):
    own = slice(TOP, TOP + rows)
    tiles = [v_ref[i, g, own] for g in range(v_ref.shape[1])]
    total = v_ref[i, 0, TOP - 1:TOP - 1 + rows] + v_ref[i, 0, TOP + 1:TOP + 1 + rows]
    total = total + (v_ref[i - 1, 0, own] + v_ref[i + 1, 0, own])
    total = total + (turned(tiles, 1, 0)[0] + turned(tiles, 127, 127)[0])
    return b_ref[i, 0, own] - (6.0 * tiles[0] - total) * (1.0 / factor)


class Exchange:
    def __init__(self, ref, sems, send, recv, box, depth, me, sizes):
        self.ref, self.sems, self.send, self.recv = ref, sems, send, recv
        self.c0, self.n, self.rows, self.l0, self.lanes = box
        self.depth, self.me, self.sizes = depth, me, sizes

    def _x(self):
        c0, n, depth = self.c0, self.n, self.depth
        gx = self.sizes[0]
        mx, my, mz = self.me
        rows = pl.ds(TOP, self.rows)
        out = []
        hop = 1
        slot = 0
        while (hop - 1) * n < depth and hop < gx:
            count = min(n, depth - (hop - 1) * n)
            far = (hop - 1) * n
            up = (c0 + n - count, c0 - far - count, mx + hop < gx, mx + hop, mx >= hop)
            down = (c0, c0 + n + far, mx >= hop, mx - hop, mx + hop < gx)
            for src, dst, may_send, peer, may_recv in (up, down):
                copy = pltpu.make_async_remote_copy(
                    src_ref=self.ref.at[pl.ds(src, count), 0, rows],
                    dst_ref=self.ref.at[pl.ds(dst, count), 0, rows],
                    send_sem=self.sems.at[0, slot],
                    recv_sem=self.sems.at[1, slot],
                    device_id=(peer, my, mz),
                    device_id_type=MESH,
                )
                out.append((copy, may_send, may_recv))
                slot += 1
            hop += 1
        return out

    def _y(self):
        gy = self.sizes[1]
        mx, my, mz = self.me
        planes = pl.ds(self.c0 - self.depth, self.n + 2 * self.depth)
        out = []
        up = (TOP + self.rows - PAD, TOP - PAD, my + 1 < gy, my + 1, my >= 1)
        down = (TOP, TOP + self.rows, my >= 1, my - 1, my + 1 < gy)
        for k, (src, dst, may_send, peer, may_recv) in enumerate((up, down)):
            copy = pltpu.make_async_remote_copy(
                src_ref=self.ref.at[planes, 0, pl.ds(src, PAD)],
                dst_ref=self.ref.at[planes, 0, pl.ds(dst, PAD)],
                send_sem=self.sems.at[0, 4 + k],
                recv_sem=self.sems.at[1, 4 + k],
                device_id=(mx, peer, mz),
                device_id_type=MESH,
            )
            out.append((copy, may_send, may_recv))
        return out

    def _z(self):
        gz = self.sizes[2]
        mx, my, mz = self.me
        out = []
        up = (0, mz + 1 < gz, mz + 1, mz >= 1)
        down = (1, mz >= 1, mz - 1, mz + 1 < gz)
        for k, may_send, peer, may_recv in (up, down):
            copy = pltpu.make_async_remote_copy(
                src_ref=self.send.at[k],
                dst_ref=self.recv.at[k],
                send_sem=self.sems.at[0, 6 + k],
                recv_sem=self.sems.at[1, 6 + k],
                device_id=(mx, my, peer),
                device_id_type=MESH,
            )
            out.append((copy, may_send, may_recv))
        return out

    def _start(self, copies):
        for copy, may_send, may_recv in copies:
            pl.when(may_send)(copy.start)

    def _wait(self, copies):
        for copy, may_send, may_recv in copies:
            pl.when(may_send)(copy.wait_send)
            pl.when(may_recv)(copy.wait_recv)

    def start_x(self):
        self._start(self._x())

    def wait_x(self):
        self._wait(self._x())

    def start_y(self):
        self._start(self._y())

    def wait_y(self):
        self._wait(self._y())

    def _planes(self):
        return range(self.c0 - self.depth, self.c0 + self.n + self.depth)

    def start_z(self):
        d = self.depth
        shape = self.send.shape[1:]
        lane = iota(shape, 1)
        up = jnp.zeros(shape, jnp.float32)
        down = jnp.zeros(shape, jnp.float32)
        for k, i in enumerate(self._planes()):
            v = self.ref[i, 0, PAD:PAD + shape[0]]
            here = (lane >= k * d) & (lane < k * d + d)
            up = jnp.where(here, pltpu.roll(v, (k * d - (self.l0 + self.lanes - d)) % 128, axis=1), up)
            down = jnp.where(here, pltpu.roll(v, (k * d - self.l0) % 128, axis=1), down)
        self.send[0] = up
        self.send[1] = down
        self._start(self._z())

    def wait_z(self):
        self._wait(self._z())
        d = self.depth
        gz = self.sizes[2]
        mz = self.me[2]
        shape = self.recv.shape[1:]
        lane = iota(shape, 1)
        low_at = (self.l0 - d) % 128
        high_at = (self.l0 + self.lanes) % 128
        is_low = (lane >= low_at) & (lane < low_at + d)
        is_high = (lane >= high_at) & (lane < high_at + d)
        low_buffer = jnp.where(mz >= 1, self.recv[0], 0.0)
        high_buffer = jnp.where(mz + 1 < gz, self.recv[1], 0.0)
        whole = self.ref.shape[1] == 2
        rows = slice(PAD, PAD + shape[0])
        for k, i in enumerate(self._planes()):
            low = pltpu.roll(low_buffer, (low_at - k * d) % 128, axis=1)
            high = pltpu.roll(high_buffer, (high_at - k * d) % 128, axis=1)
            if whole:
                self.ref[i, 1, rows] = jnp.where(is_low, low, jnp.where(is_high, high, 0.0))
            else:
                v = self.ref[i, 0, rows]
                self.ref[i, 0, rows] = jnp.where(is_low, low, jnp.where(is_high, high, v))


def kernel(
    sizes, rhs_ref, start_ref, out_ref,
    e0, b0, f0, e1, b1, f1, v2, b2, v3, b3,
    t0, t1, t2, t3, w0, w1, w2, pack, slots, side_send, side_recv,
    za, zb, zc, zd, ze, halo_sems, gather_sems,
):
    gx, gy, gz = sizes
    count = gx * gy * gz
    me = mx, my, mz = lax.axis_index("gx"), lax.axis_index("gy"), lax.axis_index("gz")
    mine = (mx * gy + my) * gz + mz
    lx, ly, lz = rhs_ref.shape
    c0, c1 = DOWN0 + 1, SIDE1 + 2
    hx, hy, hz = lx // 2, ly // 2, lz // 2
    qx, qy, qz = hx // 2, hy // 2, hz // 2
    x2, y2, z2 = gx * qx, gy * qy, gz * qz
    x3, y3, z3 = x2 // 2, y2 // 2, z2 // 2
    z3p = v3.shape[2]
    left = (128 - hz) // 2

    def coords(k):
        steps = (k // (gy * gz), k // gz % gy, k % gz)
        moved = [at + step for at, step in zip(me, steps)]
        return tuple(jnp.where(at >= size, at - size, at) for at, size in zip(moved, sizes))

    def number(at):
        return (at[0] * gy + at[1]) * gz + at[2]

    def others(body):
        if count <= 64:
            for k in range(1, count):
                body(k, 0)
        else:
            lax.fori_loop(1, count, body, 0)

    for ref in (e1, b1, f1, v2, v3):
        ref[...] = jnp.zeros_like(ref)
    for ref in (e0, b0, f0):
        n0 = ref.shape[0]
        ref[:, :, 0:TOP] = jnp.zeros((n0, 2, TOP, 128), jnp.float32)
        ref[:, :, TOP + ly:] = jnp.zeros((n0, 2, TOP, 128), jnp.float32)
        for i in list(range(c0)) + list(range(c0 + lx, n0)):
            ref[i] = jnp.zeros(ref.shape[1:], jnp.float32)

    barrier = pltpu.get_barrier_semaphore()

    def greet(k, carry):
        pl.semaphore_signal(barrier, inc=1, device_id=coords(k), device_id_type=MESH)
        return carry

    others(greet)

    e0[c0:c0 + lx, 0, TOP:TOP + ly] = start_ref[...]
    b0[c0:c0 + lx, 0, TOP:TOP + ly] = rhs_ref[...]

    def code(shape, row0, lane_of, bounds):
        y = iota(shape, 0) + row0
        z = lane_of(iota(shape, 1))
        inside = (y >= 0) & (y < bounds[0]) & (z >= 0) & (z < bounds[1])
        return jnp.where(inside, (y + z) & 1, 5)

    fine = (gy * ly, gz * lz)
    t0[0] = code(t0.shape[1:], my * ly - PAD, lambda c: mz * lz + c, fine)
    t0[1] = code(t0.shape[1:], my * ly - PAD, lambda c: mz * lz + jnp.where(c < 64, c + 128, c - 128), fine)
    t1[0] = code(t1.shape[1:], my * hy - PAD, lambda c: mz * hz + c - left, (gy * hy, gz * hz))
    t2[...] = code(t2.shape, -PAD, lambda c: c, (y2, z2))
    t3[...] = code(t3.shape, -PAD, lambda c: c, (y3, z3))

    pl.semaphore_wait(barrier, count - 1)

    box0 = (c0, lx, ly, 0, lz)
    box1 = (c1, hx, hy, left, hz)
    xe0 = Exchange(e0, halo_sems.at[0], za.at[0], za.at[1], box0, DOWN0, me, sizes)
    xb0 = Exchange(b0, halo_sems.at[1], zb.at[0], zb.at[1], box0, DOWN0 - 1, me, sizes)
    xf0 = Exchange(f0, halo_sems.at[2], zc.at[0], zc.at[1], box0, SIDE0, me, sizes)
    xb1 = Exchange(b1, halo_sems.at[3], zd.at[0], zd.at[1], box1, RHS1, me, sizes)
    xf1 = Exchange(f1, halo_sems.at[4], ze.at[0], ze.at[1], box1, SIDE1, me, sizes)

    def outer(direction, k):
        return c0 + lx - k if direction == 0 else c0 + k - 1

    def halo(direction, k):
        return c0 - k if direction == 0 else c0 + lx + k - 1

    own = slice(TOP, TOP + ly)
    checks = t0[0, PAD:PAD + ly]

    def black(i):
        return checks == lax.rem(mx * lx + (i + c0 + 1), 2)

    def merged(ref, direction, k):
        i = outer(direction, k)
        return jnp.where(black(i), ref[i, 0, own], ref[outer(direction, k + 1), 0, own])

    peers = ((mx + 1 < gx, mx + 1, mx >= 1), (mx >= 1, mx - 1, mx + 1 < gx))

    def side_copies(planes, group):
        return [
            (
                pltpu.make_async_remote_copy(
                    src_ref=side_send.at[d, planes],
                    dst_ref=side_recv.at[d, planes],
                    send_sem=halo_sems.at[group, 0, d],
                    recv_sem=halo_sems.at[group, 1, d],
                    device_id=(peer, my, mz),
                    device_id_type=MESH,
                ),
                may_send,
                may_recv,
            )
            for d, (may_send, peer, may_recv) in enumerate(peers)
        ]

    near = DOWN0 - 2
    rhs_copies = [
        (
            pltpu.make_async_remote_copy(
                src_ref=rhs_ref.at[pl.ds((lx - near, 0)[d], near)],
                dst_ref=b0.at[pl.ds((c0 - near, c0 + lx)[d], near), 0, pl.ds(TOP, ly)],
                send_sem=halo_sems.at[1, 0, d],
                recv_sem=halo_sems.at[1, 1, d],
                device_id=(peer, my, mz),
                device_id_type=MESH,
            ),
            may_send,
            may_recv,
        )
        for d, (may_send, peer, may_recv) in enumerate(peers)
    ]
    for copy, may_send, may_recv in rhs_copies:
        pl.when(may_send)(copy.start)
    for d in range(2):
        side_send[d, 0] = merged(e0, d, 1)
        side_send[d, 1] = merged(e0, d, 3)
        i = outer(d, 5)
        moved = pltpu.roll(b0[outer(d, 4), 0, own], 1, axis=0)
        side_send[d, 2] = jnp.where(black(i), e0[i, 0, own], moved)
    start_copies = side_copies(pl.ds(0, 3), 0)
    xe0._start(start_copies)
    xe0._wait(start_copies)
    for d in range(2):

        @pl.when(peers[d][2])
        def _():
            for k in range(1, 5):
                e0[halo(d, k), 0, own] = side_recv[d, (k - 1) // 2]
            e0[halo(d, 5), 0, own] = side_recv[d, 2]
            b0[halo(d, 4), 0, own] = pltpu.roll(side_recv[d, 2], ly - 1, axis=0)

    xe0.start_y()
    xb0._wait(rhs_copies)
    xb0.start_y()
    xe0.wait_y()
    xe0.start_z()
    xb0.wait_y()
    xb0.start_z()
    xe0.wait_z()
    xb0.wait_z()

    def span(c, n, depth):
        return (
            jnp.maximum(c - depth, c - mx * n),
            jnp.minimum(c + n + depth, c + (gx - mx) * n),
        )

    for step in range(4):
        first, last = span(c0, lx, 4 - step)
        fine_update(e0, b0, t0, first, last, mx * lx + c0, step % 2, 1.0, CHUNK0)

    def pair0(j, carry):
        i = c0 + 2 * j
        r = fine_residual(e0, b0, i, ly, 1.0) + fine_residual(e0, b0, i + 1, ly, 1.0)
        w0[j * ly:(j + 1) * ly, :] = r
        return carry

    for j in range(hx):
        pair0(j, 0)
    r = w0[pl.ds(0, hx * hy, stride=2), :] + w0[pl.ds(1, hx * hy, stride=2), :]
    fold = jnp.where(iota((128, 128), 1) == left + iota((128, 128), 0) // 2, 0.125, 0.0)
    r = dot(r, fold)
    for j in range(hx):
        b1[c1 + j, 0, TOP:TOP + hy] = r[j * hy:(j + 1) * hy]

    xb1.start_x()
    f0[c0:c0 + lx, 0, own] = e0[c0:c0 + lx, 0, own]
    for d in range(2):
        side_send[d, 3] = merged(f0, d, 1)
        side_send[d, 4] = merged(f0, d, 3)
    side0 = side_copies(pl.ds(3, 2), 2)
    xb1.wait_x()
    xb1.start_y()
    xb1.wait_y()
    xb1.start_z()
    xb1.wait_z()

    for step in range(4):
        first, last = span(c1, hx, 4 - step)
        fine_update(e1, b1, t1, first, last, mx * hx + c1, step % 2, 4.0, CHUNK1)

    for j in range(qx):
        i = c1 + 2 * j
        w1[j, 0:hy, :] = fine_residual(e1, b1, i, hy, 4.0) + fine_residual(e1, b1, i + 1, hy, 4.0)
    r = jnp.concatenate(
        [w1[j, pl.ds(0, qy, stride=2), :] + w1[j, pl.ds(1, qy, stride=2), :] for j in range(qx)], axis=0
    )
    tiles = qx * qy // 8
    total = None
    for t in range(tiles):
        source = iota((128, 128), 0) - left
        target = iota((128, 128), 1)
        inside = (source >= 0) & (source < hz)
        fold = jnp.where(inside & (target == t * qz + source // 2), 0.125, 0.0)
        part = dot(r[8 * t:8 * t + 8], fold)
        total = part if total is None else total + part
    pack[...] = total
    slots[mine] = total

    def gather(k):
        at = coords(k)
        d = number(at)
        return pltpu.make_async_remote_copy(
            src_ref=pack,
            dst_ref=slots.at[mine],
            send_sem=gather_sems.at[0, d],
            recv_sem=gather_sems.at[1, mine],
            device_id=at,
            device_id_type=MESH,
        )

    def gather_start(k, carry):
        gather(k).start()
        return carry

    others(gather_start)

    f1[c1:c1 + hx, 0, TOP:TOP + hy] = e1[c1:c1 + hx, 0, TOP:TOP + hy]
    xf1.start_x()
    xf0._start(side0)
    b2[...] = jnp.zeros_like(b2)
    b3[...] = jnp.zeros_like(b3)

    def gather_wait(k, carry):
        at = coords(k)
        d = number(at)
        copy = pltpu.make_async_remote_copy(
            src_ref=pack,
            dst_ref=slots.at[d],
            send_sem=gather_sems.at[0, d],
            recv_sem=gather_sems.at[1, d],
            device_id=at,
            device_id_type=MESH,
        )
        copy.wait_send()
        copy.wait_recv()
        return carry

    others(gather_wait)
    xf1.wait_x()
    xf1.start_y()
    xf0._wait(side0)
    for d in range(2):

        @pl.when(peers[d][2])
        def _():
            for k in range(1, 5):
                f0[halo(d, k), 0, own] = side_recv[d, 3 + (k - 1) // 2]

    xf0.start_y()
    per = 128 // qz

    def spread(c, carry):
        cx, cy = c // gy, lax.rem(c, gy)
        lane = iota((8, 128), 1)
        for g in range(gz // per):
            parts = [slots[c * gz + g * per + q] for q in range(per)]
            for t in range(tiles):
                p, h = t // (qy // 8), t % (qy // 8)
                tile = jnp.zeros((8, 128), jnp.float32)
                for q in range(per):
                    here = (lane >= q * qz) & (lane < (q + 1) * qz)
                    tile = jnp.where(here, pltpu.roll(parts[q], ((q - t) * qz) % 128, axis=1), tile)
                rows = pl.ds(pl.multiple_of(PAD + cy * qy + 8 * h, 8), 8)
                b2[1 + cx * qx + p, rows, 128 * g:128 * (g + 1)] = tile
        return carry

    lax.fori_loop(0, gx * gy, spread, 0)

    for step in range(4):
        update(v2, b2, t2, 1, 1 + x2, 1, step % 2, 16.0, True)

    def pair2(q, carry):
        r = residual(v2, b2, 1 + 2 * q, 16.0, True) + residual(v2, b2, 2 + 2 * q, 16.0, True)
        for g in range(z2 // 128):
            w2[g] = r[:, 128 * g:128 * (g + 1)]
        half = y2 // 2
        r = jnp.concatenate(
            [
                w2[g, pl.ds(PAD, half, stride=2), :] + w2[g, pl.ds(PAD + 1, half, stride=2), :]
                for g in range(z2 // 128)
            ],
            axis=1,
        )
        fold = jnp.where(iota((z2, z3p), 1) == iota((z2, z3p), 0) // 2, 0.125, 0.0)
        b3[1 + q, PAD:PAD + half, :] = dot(r, fold)
        return carry

    for q in range(x3):
        pair2(q, 0)
    xf0.wait_y()
    xf0.start_z()
    xf1.wait_y()
    xf1.start_z()

    def sweep3(k, planes):
        for colour in (0, 1):
            now = []
            for i in range(x3):
                total = beside(planes[i], True)
                if i > 0:
                    total = total + planes[i - 1]
                if i + 1 < x3:
                    total = total + planes[i + 1]
                value = (64.0 * b3[1 + i] + total) * SIXTH
                now.append(jnp.where(t3[...] == (i + colour) % 2, value, planes[i]))
            planes = tuple(now)
        return planes

    planes = lax.fori_loop(0, CSWEEPS, sweep3, tuple(v3[1 + i] for i in range(x3)))
    for i in range(x3):
        v3[1 + i] = planes[i]

    def lift3(q, carry):
        half = (y2 + 2 * PAD) // 2
        grow = jnp.where(iota((z3p, z2), 0) == iota((z3p, z2), 1) // 2, 1.0, 0.0)
        v = dot(v3[1 + q, PAD // 2:PAD // 2 + half, :], grow)
        for g in range(z2 // 128):
            w2[g, pl.ds(0, half, stride=2), :] = v[:, 128 * g:128 * (g + 1)]
            w2[g, pl.ds(1, half, stride=2), :] = v[:, 128 * g:128 * (g + 1)]
        for g in range(z2 // 128):
            lanes = slice(128 * g, 128 * (g + 1))
            for i in (1 + 2 * q, 2 + 2 * q):
                v2[i, :, lanes] = v2[i, :, lanes] + w2[g]
        return carry

    for q in range(x3):
        lift3(q, 0)

    for step in range(4):
        update(v2, b2, t2, 1, 1 + x2, 1, step % 2, 16.0, True)

    xf1.wait_z()
    rows1 = f1.shape[2]
    grow1 = jnp.where(
        iota((z2, 128), 0) == mz * qz + (iota((z2, 128), 1) - left + 2 * 128) // 2 - 128, 1.0, 0.0
    )
    rows2 = pl.ds(pl.multiple_of(my * qy, 8), rows1 // 2)

    high2 = rows1 // 2
    window = min(x2, qx + 2 * (SIDE1 // 2))
    begin = jnp.clip(mx * qx - SIDE1 // 2, 0, x2 - window)
    v = jnp.concatenate([v2[1 + begin + k, rows2, :] for k in range(window)], axis=0)
    v = dot(v, grow1)
    for k in range(window):
        part = v[k * high2:(k + 1) * high2]
        w1[k, pl.ds(0, high2, stride=2), :] = part
        w1[k, pl.ds(1, high2, stride=2), :] = part
    for k in range(window):
        i = c1 + 2 * (begin + k) - mx * hx
        rows = slice(PAD, rows1 - PAD)
        lifted = w1[k, rows, :]
        f1[i, 0, rows] = f1[i, 0, rows] + lifted
        f1[i + 1, 0, rows] = f1[i + 1, 0, rows] + lifted

    for step in range(4):
        first, last = span(c1, hx, 5 - step)
        fine_update(f1, b1, t1, first, last, mx * hx + c1, step % 2, 4.0, CHUNK1)

    xf0.wait_z()
    grow0 = jnp.where(
        iota((128, 256), 0) == (left + iota((128, 256), 1) // 2) % 128, 1.0, 0.0
    )
    rows0 = f0.shape[2]
    half0 = rows0 // 2

    def lift1(c, carry):
        j = first + 2 * c
        v = jnp.concatenate([f1[j + k, 0, PAD:PAD + half0] for k in range(2)], axis=0)
        v = dot(v, grow0)
        for k in range(2):
            for g in range(2):
                at = pl.ds((2 * k + g) * rows0, half0, stride=2)
                w0[at, :] = v[k * half0:(k + 1) * half0, 128 * g:128 * (g + 1)]
                at = pl.ds((2 * k + g) * rows0 + 1, half0, stride=2)
                w0[at, :] = v[k * half0:(k + 1) * half0, 128 * g:128 * (g + 1)]
        for k in range(2):
            for g in range(2):
                rows = slice(PAD, rows0 - PAD)
                base = (2 * k + g) * rows0
                lifted = w0[base + PAD:base + rows0 - PAD, :]
                for i in range(2):
                    at = c0 + 2 * (j + k - c1) + i
                    f0[at, g, rows] = f0[at, g, rows] + lifted
        return carry

    first, last = span(c1, hx, SIDE0 // 2)
    lax.fori_loop(0, (last - first) // 2, lift1, 0)

    for step in range(4):
        first, last = span(c0, lx, 3 - step)
        fine_update(f0, b0, t0, first, last, mx * lx + c0, step % 2, 1.0, CHUNK0)

    out_ref[...] = f0[c0:c0 + lx, 0, own]


def local(sizes, right_side, start):
    gx, gy, gz = sizes
    lx, ly, lz = right_side.shape
    c0, c1 = DOWN0 + 1, SIDE1 + 2
    n0, n1 = lx + 2 * c0, lx // 2 + 2 * c1
    r0, r1 = ly + 2 * TOP, ly // 2 + 2 * TOP
    x2, y2, z2 = gx * lx // 4, gy * ly // 4, gz * lz // 4
    x3, y3, z3 = x2 // 2, y2 // 2, z2 // 2
    z3p = -(-z3 // 128) * 128
    f32, i32 = jnp.float32, jnp.int32
    count = gx * gy * gz
    return pl.pallas_call(
        functools.partial(kernel, sizes),
        out_shape=jax.ShapeDtypeStruct(start.shape, f32),
        in_specs=[pl.BlockSpec(memory_space=pltpu.VMEM)] * 2,
        out_specs=pl.BlockSpec(memory_space=pltpu.VMEM),
        scratch_shapes=[
            pltpu.VMEM((n0, 2, r0, 128), f32),
            pltpu.VMEM((n0, 2, r0, 128), f32),
            pltpu.VMEM((n0, 2, r0, 128), f32),
            pltpu.VMEM((n1, 1, r1, 128), f32),
            pltpu.VMEM((n1, 1, r1, 128), f32),
            pltpu.VMEM((n1, 1, r1, 128), f32),
            pltpu.VMEM((x2 + 2, y2 + 2 * PAD, z2), f32),
            pltpu.VMEM((x2 + 2, y2 + 2 * PAD, z2), f32),
            pltpu.VMEM((x3 + 2, y3 + 2 * PAD, z3p), f32),
            pltpu.VMEM((x3 + 2, y3 + 2 * PAD, z3p), f32),
            pltpu.VMEM((2, r0 - 2 * PAD, 128), i32),
            pltpu.VMEM((1, r1 - 2 * PAD, 128), i32),
            pltpu.VMEM((y2 + 2 * PAD, z2), i32),
            pltpu.VMEM((y3 + 2 * PAD, z3p), i32),
            pltpu.VMEM((max(lx // 2 * ly, 4 * r0), 128), f32),
            pltpu.VMEM((lx // 4 + SIDE1, r1, 128), f32),
            pltpu.VMEM((z2 // 128, y2 + 2 * PAD, 128), f32),
            pltpu.VMEM((8, 128), f32),
            pltpu.VMEM((count, 8, 128), f32),
            pltpu.VMEM((2, 5, ly, 128), f32),
            pltpu.VMEM((2, 5, ly, 128), f32),
            pltpu.VMEM((2, 2, r0 - 2 * PAD, 128), f32),
            pltpu.VMEM((2, 2, r0 - 2 * PAD, 128), f32),
            pltpu.VMEM((2, 2, r0 - 2 * PAD, 128), f32),
            pltpu.VMEM((2, 2, r1 - 2 * PAD, 128), f32),
            pltpu.VMEM((2, 2, r1 - 2 * PAD, 128), f32),
            pltpu.SemaphoreType.DMA((5, 2, 8)),
            pltpu.SemaphoreType.DMA((2, count)),
        ],
        compiler_params=pltpu.CompilerParams(
            collective_id=0, has_side_effects=True, vmem_limit_bytes=60 * 1024 * 1024
        ),
    )(right_side, start)


def solution(mesh):
    sizes = (mesh.shape["gx"], mesh.shape["gy"], mesh.shape["gz"])
    spec = P("gx", "gy", "gz")
    return jax.shard_map(
        functools.partial(local, sizes), mesh=mesh, in_specs=(spec, spec), out_specs=spec, check_vma=False
    )
```

profile of v0, /device:TPU:0, one launch (start us, length us, event | category | flops | bytes accessed | tf_op | source)
XLA Modules:
  0.0 54.7 jit_solution(7031431508626805772)
XLA Ops:
  0.0 53.0 %shard_map.28 = f32[8,64,128]{2,1,0:T(8,128)} custom-call(f32[8,64,128]{2,1,0:T(8,128)} %rhs_ref.1, f32[8,64,128]{2,1,0:T(8,128)} %start_ref.1), custom_call_target="tpu_custom_call" | custom-call | tf_op jit(solution)/shard_map/pallas_call | solution.py:674
  53.0 1.7 %copy.4 = f32[8,64,128]{2,1,0:T(8,128)} copy(f32[8,64,128]{2,1,0:T(8,128)} %shard_map.28) | data formatting | bytes 524288
where the time goes:
time: 55.6 us; the launch traced here: 54.7 us
  Pallas kernels  53 us (95%)
  local copies, waits for them, and re-layouts  1.67 us (3%)
    pallas_call x1, Pallas kernels, local(): pl.pallas_call(functools.partial(kernel, sizes), out_shape=jax.ShapeDtype...  53 us
    unnamed x1, local copies, waits for them, and re-layouts  1.67 us

commit v1 on v0

v1 whole, which is shorter than its diff:
```python
import functools

import jax
import jax.numpy as jnp
from jax import lax
from jax.experimental import pallas as pl
from jax.experimental.pallas import tpu as pltpu
from jax.sharding import PartitionSpec as P

MESH = pl.DeviceIdType.MESH
SIXTH = 1.0 / 6.0
PAD = 8
TOP = 16
LANES = 128
HALO = 3
CSWEEPS = 8
REACH2 = 42
EDGE = ((0, 1, 4), (0, 2, 2), (1, 1, 3), (1, 2, 1), (2, 1, 2))
FACE = 5
RHS1 = 5
COR1 = 6
COR0 = 4


def dot(a, b):
    return jnp.dot(a, b, precision=lax.Precision.HIGHEST, preferred_element_type=jnp.float32)


def iota(shape, axis):
    return lax.broadcasted_iota(jnp.int32, shape, axis)


def turn(v, shift):
    shift %= v.shape[1]
    return pltpu.roll(v, shift, axis=1) if shift else v


def evens(rows, lanes, add=0):
    shape = (rows // 8, 8, lanes)
    return ((iota(shape, 1) + iota(shape, 2) + add) & 1).reshape(rows, lanes) == 0


def both(*terms):
    out = True
    for term in terms:
        if term is True:
            continue
        out = term if out is True else out & term
    return out


def when(condition, action):
    if condition is True:
        action()
    else:
        pl.when(condition)(action)


class Side:
    def __init__(self, hop, up, send, recv, peer):
        self.hop, self.up, self.send, self.recv, self.peer = hop, up, send, recv, peer
        self.dynamic = not isinstance(up, bool)

    def pick(self, a, b):
        if self.dynamic:
            return jnp.where(self.up, a, b)
        return a if self.up else b

    def source(self, c, n, count):
        return self.pick(c + n - count, c)

    def target(self, c, n, count):
        return self.pick(c - count, c + n)

    def landing(self, c, n, k):
        if self.dynamic:
            return jnp.where(self.up, c + n + k - 1, c - k)
        return c - k if self.up else c + n + k - 1

    def outward(self, c, n, k):
        return self.pick(c + n - k, c + k - 1)

    def base(self, c, n):
        if self.dynamic:
            return jnp.where(self.up, c + n, c - n)
        return c - self.hop * n if self.up else c + self.hop * n

    def send_shift(self):
        return self.pick(0, 1)

    def recv_shift(self):
        return jnp.where(self.up, 1, 0) if self.dynamic else (0 if self.up else 1)


class Mail:
    def __init__(self, sems):
        self.sems, self.count, self.items = sems, 0, []

    def add(self, src, dst, send, recv, peer):
        at = self.count
        self.count += 1
        copy = pltpu.make_async_remote_copy(
            src_ref=src,
            dst_ref=dst,
            send_sem=self.sems.at[0, at],
            recv_sem=self.sems.at[1, at],
            device_id=peer,
            device_id_type=MESH,
        )
        self.items.append((copy, send, recv))
        when(send, copy.start)

    def wait(self):
        for copy, send, recv in self.items:
            when(send, copy.wait_send)
            when(recv, copy.wait_recv)


def kernel(
    sizes, rhs_hbm, start_hbm, out_ref,
    rhs, start, a0, r0, f0, s0, merged_out, merged_in, zsend, zrecv, esend, erecv,
    a1, r1, b1, f1, s1, w0, w1, tiles_out, tiles_in, ysides, xysides, zout, zin,
    n_out, n_in, ny_in, nxy_in, nz_out, nz_in, g_out, g_in,
    b2r, b2b, r2, v2, pack, slots, w2, b3r, b3b, r3, v3,
    in_sems, relay, sems, gather_sems,
):
    gx, gy, gz = sizes
    count = gx * gy * gz
    mx, my, mz = lax.axis_index("gx"), lax.axis_index("gy"), lax.axis_index("gz")
    lx, ly, lz = start.shape
    n0, n1 = lx // 2, lx // 4
    hy, hz = ly // 2, lz // 2
    qy, qz = hy // 2, hz // 2
    left = (LANES - hz) // 2
    c = HALO
    y2, z2 = gy * qy, gz * qz
    p2, p3 = gx * lx // 8, gx * lx // 16
    y3, z3 = y2 // 2, z2 // 2
    z3p = r3.shape[2]
    groups0, groups1 = ly // 8, hy // 8

    copies = [
        pltpu.make_async_copy(start_hbm, start, in_sems.at[0]),
        pltpu.make_async_copy(rhs_hbm, rhs, in_sems.at[1]),
    ]
    for copy in copies:
        copy.start()

    if gx == 1:
        near, sides1 = [], []
    elif gx == 2:
        near = sides1 = [Side(1, mx == 0, True, True, 1 - mx)]
    else:
        def side(hop, up):
            if up:
                return Side(hop, True, mx + hop < gx, mx >= hop, mx + hop)
            return Side(hop, False, mx >= hop, mx + hop < gx, mx - hop)

        near = [side(1, True), side(1, False)]
        sides1 = near + [side(2, True), side(2, False)]

    def along(at, size, step):
        if step == 0:
            return True, True, at
        if step > 0:
            return at + 1 < size, at >= 1, at + 1
        return at >= 1, at + 1 < size, at - 1

    def to(side, dy, dz):
        sx, rx, px = (True, True, mx) if side is None else (side.send, side.recv, side.peer)
        sy, ry, py = along(my, gy, dy)
        sz, rz, pz = along(mz, gz, dz)
        return both(sx, sy, sz), both(rx, ry, rz), (px, py, pz)

    faces = [to(s, 0, 0) for s in near]
    faces += [to(None, d, 0) for d in (1, -1)] + [to(None, 0, d) for d in (1, -1)]

    def signal_faces(sem):
        for send, _, peer in faces:
            when(send, lambda peer=peer: pl.semaphore_signal(sem, inc=1, device_id=peer, device_id_type=MESH))

    heard = sum([(1 if recv is True else jnp.where(recv, 1, 0)) for _, recv, _ in faces])

    for ref in (zrecv, erecv, merged_in):
        ref[...] = jnp.zeros_like(ref)
    rows0 = a0.shape[3]
    for q in range(3):
        for i in range(a0.shape[1]):
            if i < c or i >= c + n0:
                a0[q, i, 0] = jnp.zeros((rows0, LANES), jnp.float32)
            else:
                a0[q, i, 0, 0:TOP] = jnp.zeros((TOP, LANES), jnp.float32)
                a0[q, i, 0, TOP + ly:] = jnp.zeros((rows0 - TOP - ly, LANES), jnp.float32)
    barrier = pltpu.get_barrier_semaphore()
    signal_faces(barrier)

    for ref in (ysides, xysides, tiles_in, zin, n_in, ny_in, nxy_in, nz_in, g_in, slots):
        ref[...] = jnp.zeros_like(ref)
    for q in range(3):
        for i in range(a0.shape[1]):
            a0[q, i, 1] = jnp.zeros((rows0, LANES), jnp.float32)
    for ref in (r0, f0):
        ref[...] = jnp.zeros_like(ref)

    def mask(shape, row0, lane_of, bounds):
        y = iota(shape, 0) + row0
        z = lane_of(iota(shape, 1))
        inside = (y >= 0) & (y < bounds[0]) & (z >= 0) & (z < bounds[1])
        return jnp.where(inside, SIXTH, 0.0)

    fine = (gy * ly, gz * lz)
    s0[0] = mask(s0.shape[1:], my * ly - PAD, lambda k: mz * lz + k, fine)
    s0[1] = mask(s0.shape[1:], my * ly - PAD, lambda k: mz * lz + jnp.where(k < 64, k + lz, k - LANES), fine)
    s1[0] = mask(s1.shape[1:], my * hy - PAD, lambda k: mz * hz + k - left, (gy * hy, gz * hz))

    own = slice(TOP, TOP + ly)
    even = evens(ly, LANES)
    for copy in copies:
        copy.wait()
    for i in range(n0):
        a0[0, c + i, 0, own] = jnp.where(even, start[2 * i + 1], start[2 * i])
        a0[1, c + i, 0, own] = jnp.where(even, rhs[2 * i], rhs[2 * i + 1])
        a0[2, c + i, 0, own] = jnp.where(even, rhs[2 * i + 1], rhs[2 * i])
    for s, side in enumerate(near):
        third = a0[0, side.outward(c, n0, 3), 0, own]
        second = a0[2, side.outward(c, n0, 2), 0, own]
        merged_out[s] = jnp.where(evens(ly, LANES, side.send_shift()), third, pltpu.roll(second, 1, axis=0))

    pl.semaphore_wait(barrier, heard)

    lane64 = iota((ly, LANES), 1)
    lane8 = iota((8, LANES), 1)
    ydirs = zdirs = (1, -1)
    mail = Mail(sems.at[0])
    for s, side in enumerate(near):
        where = to(side, 0, 0)
        src, dst = side.source(c, n0, 2), side.target(c, n0, 2)
        mail.add(a0.at[0:2, pl.ds(src, 2), 0, own], a0.at[0:2, pl.ds(dst, 2), 0, own], *where)
        src, dst = side.source(c, n0, 1), side.target(c, n0, 1)
        mail.add(a0.at[2, pl.ds(src, 1), 0, own], a0.at[2, pl.ds(dst, 1), 0, own], *where)
        mail.add(merged_out.at[s], merged_in.at[s], *where)

    def strip(d, rows):
        return (TOP + rows - 8, TOP - 8) if d > 0 else (TOP, TOP + rows)

    for d in ydirs:
        src, dst = strip(d, ly)
        mail.add(
            a0.at[0:3, pl.ds(c, n0), 0, pl.ds(src, 8)], a0.at[0:3, pl.ds(c, n0), 0, pl.ds(dst, 8)], *to(None, d, 0)
        )
    signal_faces(relay.at[0])

    slots0 = [(q, i) for i in range(n0) for q in range(3)]
    for zi, d in enumerate(zdirs):
        packed = jnp.zeros((ly, LANES), jnp.float32)
        for t, (q, i) in enumerate(slots0):
            v = a0[q, c + i, 0, own]
            first = lz - FACE if d > 0 else 0
            here = (lane64 >= FACE * t) & (lane64 < FACE * (t + 1))
            packed = jnp.where(here, turn(v, FACE * t - first), packed)
        zsend[zi] = packed
    for zi, d in enumerate(zdirs):
        mail.add(zsend.at[zi], zrecv.at[zi, pl.ds(8, ly)], *to(None, 0, d))

    width = sum(w for _, _, w in EDGE)
    starts = [sum(w for _, _, w in EDGE[:t]) for t in range(len(EDGE))]
    for s, side in enumerate(near):
        for zi, d in enumerate(zdirs):
            packed = jnp.zeros((8, LANES), jnp.float32)
            for (q, k, w), at in zip(EDGE, starts):
                v = a0[q, side.outward(c, n0, k), 0, own]
                for g in range(groups0):
                    lo = width * g + at
                    first = lz - w if d > 0 else 0
                    here = (lane8 >= lo) & (lane8 < lo + w)
                    packed = jnp.where(here, turn(v[8 * g:8 * g + 8], lo - first), packed)
            esend[s, zi] = packed
    pl.semaphore_wait(relay.at[0], heard)
    signal_faces(relay.at[1])
    for s, side in enumerate(near):
        p_src, p_dst = side.source(c, n0, 2), side.target(c, n0, 2)
        for d in ydirs:
            src, dst = strip(d, ly)
            mail.add(
                a0.at[0:3, pl.ds(p_src, 2), 0, pl.ds(src, 8)],
                a0.at[0:3, pl.ds(p_dst, 2), 0, pl.ds(dst, 8)],
                *to(side, d, 0),
            )
    for zi, dz in enumerate(zdirs):
        for d in ydirs:
            src, dst = strip(d, ly)
            mail.add(
                zsend.at[zi, pl.ds(src - TOP, 8)], zrecv.at[zi, pl.ds(dst - 8, 8)], *to(None, d, dz)
            )
        for s, side in enumerate(near):
            mail.add(esend.at[s, zi], erecv.at[s, zi, 1], *to(side, 0, dz))
    rounds = relay.shape[0]
    pl.semaphore_wait(relay.at[1], heard)
    for zi, dz in enumerate(zdirs):
        for s, side in enumerate(near):
            for d in ydirs:
                mail.add(esend.at[s, zi], erecv.at[s, zi, 0 if d > 0 else 2], *to(side, d, dz))
    for r in range(2, rounds):
        signal_faces(relay.at[r])
        pl.semaphore_wait(relay.at[r], heard)
    mail.wait()

    for s, side in enumerate(near):
        v = merged_in[s]
        a0[0, side.landing(c, n0, 3), 0, own] = v
        a0[2, side.landing(c, n0, 2), 0, own] = pltpu.roll(v, ly - 1, axis=0)
    rows_h = ly + 16
    lane_h = iota((rows_h, LANES), 1)
    for t, (q, i) in enumerate(slots0):
        low = turn(zrecv[0], LANES - FACE - FACE * t)
        high = turn(zrecv[1], -FACE * t)
        a0[q, c + i, 1, PAD:PAD + rows_h] = jnp.where(
            lane_h >= LANES - FACE, low, jnp.where(lane_h < FACE, high, 0.0)
        )
    for s, side in enumerate(near):
        for (q, k, w), at in zip(EDGE, starts):
            pair = side.landing(c, n0, k)
            for g in range(groups0 + 2):
                which, group = (0, groups0 - 1) if g == 0 else ((2, 0) if g > groups0 else (1, g - 1))
                lo = width * group + at
                low = turn(erecv[s, 0, which], LANES - w - lo)
                high = turn(erecv[s, 1, which], -lo)
                a0[q, pair, 1, PAD + 8 * g:PAD + 8 * g + 8] = jnp.where(
                    lane8 >= LANES - w, low, jnp.where(lane8 < w, high, 0.0)
                )

    def span(n, k):
        if gx == 1:
            return c, n
        k = min(k, n * (gx - 1), HALO)
        if gx == 2:
            return jnp.where(mx == 0, c, c - k), n + k
        return c - k, n + 2 * k

    def inside(n, i):
        if gx <= 2:
            return None
        at = mx * n + i - c
        return jnp.where((at >= 0) & (at < gx * n), 1.0, 0.0)

    def neighbours(src, i, planes, red, chess, lo, hi, tiles):
        prev, cur, nxt = planes
        low = [turn(t, 1) for t in cur]
        high = [turn(t, -1) for t in cur]
        if len(cur) == 2:
            lane = iota(cur[0].shape, 1)
            low = [jnp.where(lane == 0, low[1 - g], low[g]) for g in range(tiles)]
            high = [jnp.where(lane == LANES - 1, high[1 - g], high[g]) for g in range(tiles)]
        out = []
        for g in range(tiles):
            beside = jnp.where(chess, prev[g], nxt[g]) if red else jnp.where(chess, nxt[g], prev[g])
            total = (cur[g] + beside) + (src[i, g, lo - 1:hi - 1] + src[i, g, lo + 1:hi + 1])
            out.append(total + (low[g] + high[g]))
        return out

    def relax(dst, src, rhs_of, scale, n, k, red, factor, tiles=None, emit=None):
        first, length = span(n, k)
        held = src.shape[1]
        rows = src.shape[2]
        lo, hi = (TOP, rows - TOP) if emit else (PAD, rows - PAD)
        tiles = tiles or held
        chess = evens(hi - lo, LANES)
        planes = [[src[first + j - 1, g, lo:hi] for g in range(held)] for j in range(length + 2)]
        for j in range(length):
            i = first + j
            totals = neighbours(src, i, planes[j:j + 3], red, chess, lo, hi, tiles)
            factor_x = inside(n, i)
            for g in range(tiles):
                b = rhs_of(i, g, lo, hi)
                if factor != 1.0:
                    b = b * factor
                value = (b + totals[g]) * scale[g, lo - PAD:hi - PAD]
                if factor_x is not None:
                    value = value * factor_x
                if emit:
                    emit(j, planes[j + 1][g], value)
                else:
                    dst[i, g, lo:hi] = value

    def residual(red_ref, black_ref, red_rhs, black_rhs, n, j, factor):
        rows = red_ref.shape[2]
        lo, hi = TOP, rows - TOP
        chess = evens(hi - lo, LANES)
        i = c + j
        held = red_ref.shape[1]

        def load(ref):
            return [[ref[i + d, g, lo:hi] for g in range(held if d == 0 else 1)] for d in (-1, 0, 1)]

        red, black = load(red_ref), load(black_ref)
        from_black = neighbours(black_ref, i, black, True, chess, lo, hi, 1)[0]
        from_red = neighbours(red_ref, i, red, False, chess, lo, hi, 1)[0]
        out = red_rhs(i, 0, lo, hi) - (6.0 * red[1][0] - from_black) * (1.0 / factor)
        return out + (black_rhs(i, 0, lo, hi) - (6.0 * black[1][0] - from_red) * (1.0 / factor))

    black0 = a0.at[0]
    rhs0 = [lambda i, g, lo, hi, q=q: a0[q, i, g, lo:hi] for q in (1, 2)]
    for step in range(4):
        k = (4 - step + 1) // 2
        if step % 2 == 0:
            relax(r0, black0, rhs0[0], s0, n0, k, True, 1.0)
        else:
            relax(black0, r0, rhs0[1], s0, n0, k, False, 1.0)
    for j in range(n0):
        w0[j * ly:(j + 1) * ly, :] = residual(r0, black0, rhs0[0], rhs0[1], n0, j, 1.0)
    r = w0[pl.ds(0, n0 * hy, stride=2), :] + w0[pl.ds(1, n0 * hy, stride=2), :]
    source, target = iota((LANES, LANES), 0), iota((LANES, LANES), 1)
    fold = jnp.where(lax.rem(target - left + LANES, hz) == source // 2, 0.125, 0.0)
    r = dot(r, fold)

    own1 = slice(TOP, TOP + hy)
    lane32 = iota((hy, LANES), 1)
    mid = (lane32 >= left) & (lane32 < left + hz)
    chess1 = evens(hy, LANES)
    for j in range(n1):
        one, two = r[2 * j * hy:(2 * j + 1) * hy], r[(2 * j + 1) * hy:(2 * j + 2) * hy]
        red = jnp.where(chess1, one, two)
        black = jnp.where(chess1, two, one)
        tiles_out[j] = jnp.where(mid, red, black)
        a1[0, c + j, 0, own1] = jnp.where(mid, red, 0.0)
        a1[1, c + j, 0, own1] = jnp.where(mid, black, 0.0)

    def pack_edges(read, items, w):
        for d in zdirs:
            first = left + hz - w if d > 0 else left
            packed = jnp.zeros((8, LANES), jnp.float32)
            for t in range(items * groups1):
                here = (lane8 >= w * t) & (lane8 < w * (t + 1))
                packed = jnp.where(here, turn(read(t), w * t - first), packed)
            yield packed

    def post1(mail, out, into, y_in, xy_in, z_out, z_in):
        for s, side in enumerate(sides1):
            mail.add(out, into.at[s], *to(side, 0, 0))
        for yi, d in enumerate(ydirs):
            src = hy - 8 if d > 0 else 0
            mail.add(out.at[:, pl.ds(src, 8)], y_in.at[yi], *to(None, d, 0))
        for s, side in enumerate(sides1):
            for yi, d in enumerate(ydirs):
                src = hy - 8 if d > 0 else 0
                mail.add(out.at[:, pl.ds(src, 8)], xy_in.at[s, yi], *to(side, d, 0))
        for zi, dz in enumerate(zdirs):
            for s, side in enumerate([None] + sides1):
                for yi, d in enumerate((1, 0, -1)):
                    mail.add(z_out.at[zi], z_in.at[zi, s, yi], *to(side, d, dz))

    def regions1():
        yield from ((None, None, j, c + j) for j in range(n1))
        for s, side in enumerate(sides1):
            for j in range(n1):
                at = side.base(c, n1) + j
                if side.dynamic or 0 <= at < 2 * c + n1:
                    yield (s, side, j, at)

    def row_groups():
        yield 0, groups1 - 1, None, 0
        for g in range(groups1):
            yield 1, g, g, None
        yield 2, 0, None, 1

    lane_l = lane8
    mid8 = (lane_l >= left) & (lane_l < left + hz)

    def edges(z_in, s, which, lo, w):
        at = 0 if s is None else s + 1
        low = turn(z_in[0, at, which], left - w - lo)
        high = turn(z_in[1, at, which], left + hz - lo)
        return jnp.where(lane_l < left, low, high)

    items = 2 * n1
    order1 = [(g, q, j) for g in range(groups1) for j in range(n1) for q in range(2)]
    tile_of = lambda t: a1[order1[t][1], c + order1[t][2], 0, TOP + 8 * order1[t][0]:TOP + 8 * order1[t][0] + 8]
    for zi, packed in enumerate(pack_edges(tile_of, items, RHS1)):
        zout[zi] = packed
    mail = Mail(sems.at[1])
    post1(mail, tiles_out, tiles_in, ysides, xysides, zout, zin)
    for ref in (a1, r1, b1, f1):
        for i in range(ref.shape[-4]):
            halo_pair = i < c or i >= c + n1
            lead = (slice(None),) if len(ref.shape) == 5 else ()
            if halo_pair or ref is not a1:
                at = lead + (i,)
                ref[at] = jnp.zeros(ref[at].shape, jnp.float32)
            else:
                for rows in (slice(0, TOP), slice(TOP + hy, None)):
                    at = lead + (i, slice(None), rows)
                    ref[at] = jnp.zeros(ref[at].shape, jnp.float32)
    for ref in (b2r, b2b, r2, v2, b3r, b3b, r3, v3):
        ref[...] = jnp.zeros_like(ref)
    mail.wait()

    near_lanes = (lane_l >= left - RHS1) & (lane_l < left + hz + RHS1)
    for s, side, j, at in regions1():
        for n, (which, group, rows, yi) in enumerate(row_groups()):
            if rows is None:
                base = ysides[yi, j] if s is None else xysides[s, yi, j]
            elif s is None:
                base = None
            else:
                base = tiles_in[s, j, 8 * rows:8 * rows + 8]
            for q in range(2):
                to_rows = slice(PAD + 8 * n, PAD + 8 * n + 8)
                lo = RHS1 * ((group * n1 + j) * 2 + q)
                if base is None:
                    middle = a1[q, at, 0, to_rows]
                else:
                    middle = base if q == 0 else turn(base, LANES - hz)
                outer = edges(zin, s, which, lo, RHS1)
                a1[q, at, 0, to_rows] = jnp.where(mid8, middle, jnp.where(near_lanes, outer, 0.0))

    rhs1 = [lambda i, g, lo, hi, q=q: a1[q, i, g, lo:hi] for q in (0, 1)]
    first, length = span(n1, 2)
    for j in range(length):
        i = first + j
        value = (a1[0, i, 0, PAD:-PAD] * 4.0) * s1[0]
        factor_x = inside(n1, i)
        r1[i, 0, PAD:-PAD] = value if factor_x is None else value * factor_x
    relax(b1, r1, rhs1[1], s1, n1, 2, False, 4.0)
    relax(r1, b1, rhs1[0], s1, n1, 1, True, 4.0)
    relax(b1, r1, rhs1[1], s1, n1, 1, False, 4.0)

    for j in range(n1):
        w1[j, 0:hy, :] = residual(r1, b1, rhs1[0], rhs1[1], n1, j, 4.0)
    r = jnp.concatenate(
        [w1[j, pl.ds(0, qy, stride=2), :] + w1[j, pl.ds(1, qy, stride=2), :] for j in range(n1)], axis=0
    )
    fold = jnp.where(
        (lax.rem(target, qz) == (source - left) // 2) & (source >= left) & (source < left + hz), 0.125, 0.0
    )
    r = dot(r, fold)
    block = lane8 // qz
    per_colour = qy // 8
    one = two = None
    for h in range(per_colour):
        p, q = r[8 * h:8 * h + 8], r[qy + 8 * h:qy + 8 * h + 8]
        here = lax.rem(block, per_colour) == h
        one = p if one is None else jnp.where(here, p, one)
        two = q if two is None else jnp.where(here, q, two)
    tile = jnp.where(evens(8, LANES) ^ (block >= per_colour), one, two)
    pack[...] = tile

    mine = (mx * gy + my) * gz + mz
    slots[mine] = tile

    dist = (-(-REACH2 // (lx // 4)), -(-REACH2 // qy), -(-REACH2 // qz))

    def coords(k):
        steps = (k // (gy * gz), k // gz % gy, k % gz)
        moved = [at + step for at, step in zip((mx, my, mz), steps)]
        at = tuple(jnp.where(v >= size, v - size, v) for v, size in zip(moved, sizes))
        close = True
        for a, b, size, reach in zip(at, (mx, my, mz), sizes, dist):
            if reach < size - 1:
                close = both(close, (a - b <= reach) & (b - a <= reach))
        return at, close

    def number(at):
        return (at[0] * gy + at[1]) * gz + at[2]

    def others(body):
        if count <= 64:
            for k in range(1, count):
                body(k)
        else:
            def step(k, carry):
                body(k)
                return carry

            lax.fori_loop(1, count, step, 0)

    def gather(k, arriving):
        at, close = coords(k)
        d = number(at)
        return pltpu.make_async_remote_copy(
            src_ref=pack,
            dst_ref=slots.at[d if arriving else mine],
            send_sem=gather_sems.at[0, d],
            recv_sem=gather_sems.at[1, d if arriving else mine],
            device_id=at,
            device_id_type=MESH,
        ), close

    def gather_start(k):
        copy, close = gather(k, False)
        when(close, copy.start)

    def gather_wait(k):
        copy, close = gather(k, True)

        def done():
            copy.wait_send()
            copy.wait_recv()

        when(close, done)

    others(gather_start)

    red_out = jnp.where(mid, b1[c, 0, own1], turn(b1[c + n1 - 1, 0, own1], LANES - hz))
    n_out[0] = red_out
    order_n = [(g, j) for g in range(groups1) for j in range(n1)]
    tile_n = lambda t: b1[c + order_n[t][1], 0, TOP + 8 * order_n[t][0]:TOP + 8 * order_n[t][0] + 8]
    for zi, packed in enumerate(pack_edges(tile_n, n1, COR1)):
        nz_out[zi] = packed
    mail1 = Mail(sems.at[2])
    post1(mail1, n_out, n_in, ny_in, nxy_in, nz_out, nz_in)

    for zi, d in enumerate(zdirs):
        packed = jnp.zeros((8, LANES), jnp.float32)
        for i in range(n0):
            v = a0[0, c + i, 0, own]
            for g in range(groups0):
                lo = COR0 * (g * n0 + i)
                first = lz - COR0 if d > 0 else 0
                here = (lane8 >= lo) & (lane8 < lo + COR0)
                packed = jnp.where(here, turn(v[8 * g:8 * g + 8], lo - first), packed)
        g_out[zi] = packed
    mail0 = Mail(sems.at[3])
    for side in near:
        src, dst = side.source(c, n0, 2), side.target(c, n0, 2)
        mail0.add(black0.at[pl.ds(src, 2), 0, own], f0.at[pl.ds(dst, 2), 0, own], *to(side, 0, 0))
        for d in ydirs:
            ysrc, ydst = strip(d, ly)
            mail0.add(
                black0.at[pl.ds(src, 2), 0, pl.ds(ysrc, 8)], f0.at[pl.ds(dst, 2), 0, pl.ds(ydst, 8)], *to(side, d, 0)
            )
    for d in ydirs:
        ysrc, ydst = strip(d, ly)
        mail0.add(
            black0.at[pl.ds(c, n0), 0, pl.ds(ysrc, 8)], f0.at[pl.ds(c, n0), 0, pl.ds(ydst, 8)], *to(None, d, 0)
        )
    for zi, dz in enumerate(zdirs):
        for s, side in enumerate([None] + near):
            for yi, d in enumerate((1, 0, -1)):
                mail0.add(g_out.at[zi], g_in.at[zi, s, yi], *to(side, d, dz))

    others(gather_wait)

    per = LANES // qz
    for k in range(gx * gy):
        cx, cy = k // gy, k % gy
        for g in range(gz // per):
            parts = [slots[k * gz + g * per + q] for q in range(per)]
            for h in range(per_colour):
                for colour, ref in ((0, b2r), (1, b2b)):
                    at = colour * per_colour + h
                    v = None
                    for q in range(per):
                        moved = turn(parts[q], (q - at) * qz)
                        here = (lane8 >= q * qz) & (lane8 < (q + 1) * qz)
                        v = moved if v is None else jnp.where(here, moved, v)
                    ref[1 + cx, PAD + cy * qy + 8 * h:PAD + cy * qy + 8 * h + 8, LANES * g:LANES * (g + 1)] = v

    def coarse_total(src, i, red, rows, full):
        width_z = src.shape[2]
        lo, hi = PAD, PAD + rows
        v = src[i, lo:hi]
        low, high = turn(v, 1), turn(v, -1)
        lane = iota(v.shape, 1)
        if full:
            low = jnp.where(lane == 0, 0.0, low)
            high = jnp.where(lane == width_z - 1, 0.0, high)
        chess = evens(rows, width_z)
        prev, nxt = src[i - 1, lo:hi], src[i + 1, lo:hi]
        beside = jnp.where(chess, prev, nxt) if red else jnp.where(chess, nxt, prev)
        total = (v + beside) + (src[i, lo - 1:hi - 1] + src[i, lo + 1:hi + 1])
        return v, total + (low + high)

    def coarse(dst, src, b, pairs, red, factor, rows, scale, full):
        for i in range(1, pairs + 1):
            _, total = coarse_total(src, i, red, rows, full)
            dst[i, PAD:PAD + rows] = (b[i, PAD:PAD + rows] * factor + total) * scale

    in2 = slice(PAD, PAD + y2)
    for i in range(1, p2 + 1):
        r2[i, in2] = (b2r[i, in2] * 16.0) * SIXTH
    coarse(v2, r2, b2b, p2, False, 16.0, y2, SIXTH, True)
    coarse(r2, v2, b2r, p2, True, 16.0, y2, SIXTH, True)
    coarse(v2, r2, b2b, p2, False, 16.0, y2, SIXTH, True)

    fold = jnp.where(iota((z2, z3p), 1) == iota((z2, z3p), 0) // 2, 0.125, 0.0)
    parts = []
    for i in range(1, p2 + 1):
        red, from_black = r2[i, in2], coarse_total(v2, i, True, y2, True)[1]
        black, from_red = v2[i, in2], coarse_total(r2, i, False, y2, True)[1]
        r = b2r[i, in2] - (6.0 * red - from_black) * 0.0625
        r = r + (b2b[i, in2] - (6.0 * black - from_red) * 0.0625)
        for g in range(z2 // LANES):
            w2[i - 1, g, 0:y2] = r[:, LANES * g:LANES * (g + 1)]
        parts.append(
            jnp.concatenate(
                [
                    w2[i - 1, g, pl.ds(0, y3, stride=2), :] + w2[i - 1, g, pl.ds(1, y3, stride=2), :]
                    for g in range(z2 // LANES)
                ],
                axis=1,
            )
        )
    r = dot(jnp.concatenate(parts, axis=0), fold)
    chess3 = evens(y3, z3p)
    in3 = slice(PAD, PAD + y3)
    for j in range(p3):
        one, two = r[2 * j * y3:(2 * j + 1) * y3], r[(2 * j + 1) * y3:(2 * j + 2) * y3]
        b3r[1 + j, in3] = jnp.where(chess3, one, two)
        b3b[1 + j, in3] = jnp.where(chess3, two, one)

    full3 = z3 == z3p
    scale3 = SIXTH if full3 else jnp.where(iota((y3, z3p), 1) < z3, SIXTH, 0.0)

    def sweep3(_, carry):
        coarse(r3, v3, b3r, p3, True, 64.0, y3, scale3, full3)
        coarse(v3, r3, b3b, p3, False, 64.0, y3, scale3, full3)
        return carry

    if p3 == 1:
        for _ in range(CSWEEPS):
            sweep3(0, 0)
    else:
        lax.fori_loop(0, CSWEEPS, sweep3, 0)

    def plane(red, black, chess, odd):
        return jnp.where(chess, black, red) if odd else jnp.where(chess, red, black)

    grow = jnp.where(iota((z3p, z2), 0) == iota((z3p, z2), 1) // 2, 1.0, 0.0)
    v = jnp.concatenate(
        [plane(r3[1 + i // 2, in3], v3[1 + i // 2, in3], chess3, i % 2) for i in range(p2)], axis=0
    )
    v = dot(v, grow)
    for i in range(p2):
        part = v[i * y3:(i + 1) * y3]
        for g in range(z2 // LANES):
            w2[i, g, pl.ds(0, y3, stride=2), :] = part[:, LANES * g:LANES * (g + 1)]
            w2[i, g, pl.ds(1, y3, stride=2), :] = part[:, LANES * g:LANES * (g + 1)]
    for i in range(p2):
        for g in range(z2 // LANES):
            lanes = slice(LANES * g, LANES * (g + 1))
            v2[1 + i, in2, lanes] = v2[1 + i, in2, lanes] + w2[i, g, 0:y2]
    for _ in range(2):
        coarse(r2, v2, b2r, p2, True, 16.0, y2, SIXTH, True)
        coarse(v2, r2, b2b, p2, False, 16.0, y2, SIXTH, True)

    mail1.wait()
    grow1 = jnp.where(
        iota((z2, LANES), 0) == mz * qz + (iota((z2, LANES), 1) - left + 2 * LANES) // 2 - LANES, 1.0, 0.0
    )
    rows1 = f1.shape[2]
    half1 = rows1 // 2
    rows2 = pl.ds(pl.multiple_of(my * qy, 8), half1)
    chess2 = evens(half1, z2)
    first, length = span(n1, HALO)
    begin = first - c + mx * n1
    shift = 0 if gx <= 2 else 1
    first_even = begin - shift
    tops = []
    for j in range(length):
        at = j + shift
        index = (first_even + (at - at % 2)) // 2 + 1
        if gx > 2:
            index = jnp.clip(index, 0, p2 + 1)
        tops.append(plane(r2[index, rows2], v2[index, rows2], chess2, at % 2))
    v = dot(jnp.concatenate(tops, axis=0), grow1)
    for j in range(length):
        part = v[j * half1:(j + 1) * half1]
        w1[j, pl.ds(0, half1, stride=2), :] = part
        w1[j, pl.ds(1, half1, stride=2), :] = part

    near_lanes = (lane_l >= left - COR1) & (lane_l < left + hz + COR1)
    for s, side, j, at in regions1():
        for n, (which, group, rows, yi) in enumerate(row_groups()):
            to_rows = slice(PAD + 8 * n, PAD + 8 * n + 8)
            if rows is None:
                base = ny_in[yi, 0] if s is None else nxy_in[s, yi, 0]
            elif s is None:
                base = None
            else:
                base = n_in[s, 0, 8 * rows:8 * rows + 8]
            if base is None:
                middle = b1[at, 0, to_rows]
            else:
                middle = base if j == 0 else turn(base, LANES - hz)
            outer = edges(nz_in, s, which, COR1 * (group * n1 + j), COR1)
            value = jnp.where(mid8, middle, jnp.where(near_lanes, outer, 0.0))
            f1[at, 0, to_rows] = value + w1[at - first, to_rows, :]

    for step in range(4):
        k = (5 - step + 1) // 2
        if step % 2 == 0:
            relax(r1, f1, rhs1[0], s1, n1, k, True, 4.0)
        else:
            relax(f1, r1, rhs1[1], s1, n1, k, False, 4.0)

    mail0.wait()
    grow0 = jnp.where(
        iota((LANES, 2 * LANES), 0) == (left + iota((LANES, 2 * LANES), 1) // 2) % LANES, 1.0, 0.0
    )
    half0 = rows0 // 2
    first, length = span(n0, 2)
    chess_h = evens(half0, LANES)
    tops = []
    for j in range(length):
        index = (first - c + j - j % 2) // 2 + c if gx <= 2 else (first - c + j) // 2 + c
        red, black = r1[index, 0, PAD:PAD + half0], f1[index, 0, PAD:PAD + half0]
        tops.append(plane(red, black, chess_h, j % 2))
    v = dot(jnp.concatenate(tops, axis=0), grow0)
    for j in range(length):
        for g in range(2):
            base = (2 * j + g) * rows0
            part = v[j * half0:(j + 1) * half0, LANES * g:LANES * (g + 1)]
            w0[pl.ds(base, half0, stride=2), :] = part
            w0[pl.ds(base + 1, half0, stride=2), :] = part

    for i in range(n0):
        at = c + i
        j = at - first
        lift = w0[pl.ds(pl.multiple_of(2 * j * rows0, 8) + TOP, ly), :]
        f0[at, 0, own] = black0[at, 0, own] + lift
        for rows in (slice(PAD, TOP), slice(TOP + ly, TOP + ly + 8)):
            lift = w0[pl.ds(pl.multiple_of(2 * j * rows0, 8) + rows.start, 8), :]
            f0[at, 0, rows] = f0[at, 0, rows] + lift
    for side in near:
        for k in (1, 2):
            at = side.landing(c, n0, k)
            j = at - first
            lift = w0[pl.ds(pl.multiple_of(2 * j * rows0, 8) + PAD, rows_h), :]
            f0[at, 0, PAD:PAD + rows_h] = f0[at, 0, PAD:PAD + rows_h] + lift
    for s, side in enumerate([None] + near):
        pairs = range(n0) if side is None else (1, 2)
        for k in pairs:
            if side is None:
                at, far = c + k, k
            else:
                at = side.landing(c, n0, k)
                far = None
            for n in range(groups0 + 2):
                which, group = (0, groups0 - 1) if n == 0 else ((2, 0) if n > groups0 else (1, n - 1))
                tiles = []
                for zi in range(2):
                    t = g_in[zi, s, which]
                    if far is not None:
                        lo = COR0 * (group * n0 + far)
                        tiles.append(turn(t, (LANES - COR0 if zi == 0 else 0) - lo))
                    elif side.dynamic:
                        spot = (LANES - COR0 if zi == 0 else 0)
                        a = turn(t, spot - COR0 * (group * n0 + k - 1))
                        b = turn(t, spot - COR0 * (group * n0 + n0 - k))
                        tiles.append(jnp.where(side.up, a, b))
                    else:
                        far_at = n0 - k if side.up else k - 1
                        tiles.append(turn(t, (LANES - COR0 if zi == 0 else 0) - COR0 * (group * n0 + far_at)))
                low, high = tiles
                value = jnp.where(lane8 >= LANES - COR0, low, jnp.where(lane8 < COR0, high, 0.0))
                j = at - first
                to_rows = slice(PAD + 8 * n, PAD + 8 * n + 8)
                lift = w0[pl.ds(pl.multiple_of((2 * j + 1) * rows0, 8) + PAD + 8 * n, 8), :]
                f0[at, 1, to_rows] = value + lift

    relax(r0, f0, rhs0[0], s0, n0, 2, True, 1.0)
    relax(f0, r0, rhs0[1], s0, n0, 1, False, 1.0)
    relax(r0, f0, rhs0[0], s0, n0, 1, True, 1.0)

    def emit(j, red, black):
        out_ref[2 * j] = jnp.where(even, red, black)
        out_ref[2 * j + 1] = jnp.where(even, black, red)

    relax(None, r0, rhs0[1], s0, n0, 0, False, 1.0, tiles=1, emit=emit)


def local(sizes, right_side, start):
    gx, gy, gz = sizes
    lx, ly, lz = start.shape
    f32 = jnp.float32
    count = gx * gy * gz
    near = {1: 0, 2: 1}.get(gx, 2)
    far = {1: 0, 2: 1}.get(gx, 4)
    n0, n1 = lx // 2, lx // 4
    m0, m1 = n0 + 2 * HALO, n1 + 2 * HALO
    r0, r1 = ly + 2 * TOP, ly // 2 + 2 * TOP
    hy = ly // 2
    y2, z2 = gy * ly // 4, gz * lz // 4
    p2, p3 = gx * lx // 8, gx * lx // 16
    y3, z3 = y2 // 2, z2 // 2
    z3p = -(-z3 // LANES) * LANES
    dx = min(gx - 1, -(-REACH2 // (lx // 4)))
    dy = min(gy - 1, -(-REACH2 // (ly // 4)))
    dz = min(gz - 1, -(-REACH2 // (lz // 4)))
    rounds = max(2, sum(max(0, d - 2) for d in (dx, dy, dz)) - 1)
    near_a, far_a = max(near, 1), max(far, 1)

    def vmem(*shape):
        return pltpu.VMEM(shape, f32)

    messages = 24 if gx <= 2 else 48
    return pl.pallas_call(
        functools.partial(kernel, sizes),
        out_shape=jax.ShapeDtypeStruct(start.shape, f32),
        in_specs=[pl.BlockSpec(memory_space=pl.ANY)] * 2,
        out_specs=pl.BlockSpec(memory_space=pltpu.VMEM),
        scratch_shapes=[
            vmem(lx, ly, lz),
            vmem(lx, ly, lz),
            vmem(3, m0, 2, r0, LANES),
            vmem(m0, 2, r0, LANES),
            vmem(m0, 2, r0, LANES),
            vmem(2, r0 - 2 * PAD, LANES),
            vmem(near_a, ly, LANES),
            vmem(near_a, ly, LANES),
            vmem(2, ly, LANES),
            vmem(2, ly + 16, LANES),
            vmem(near_a, 2, 8, LANES),
            vmem(near_a, 2, 3, 8, LANES),
            vmem(2, m1, 1, r1, LANES),
            vmem(m1, 1, r1, LANES),
            vmem(m1, 1, r1, LANES),
            vmem(m1, 1, r1, LANES),
            vmem(1, r1 - 2 * PAD, LANES),
            vmem(2 * m0 * r0, LANES),
            vmem(m1, r1, LANES),
            vmem(n1, hy, LANES),
            vmem(far_a, n1, hy, LANES),
            vmem(2, n1, 8, LANES),
            vmem(far_a, 2, n1, 8, LANES),
            vmem(2, 8, LANES),
            vmem(2, far + 1, 3, 8, LANES),
            vmem(1, hy, LANES),
            vmem(far_a, 1, hy, LANES),
            vmem(2, 1, 8, LANES),
            vmem(far_a, 2, 1, 8, LANES),
            vmem(2, 8, LANES),
            vmem(2, far + 1, 3, 8, LANES),
            vmem(2, 8, LANES),
            vmem(2, near + 1, 3, 8, LANES),
            vmem(p2 + 2, y2 + 2 * PAD, z2),
            vmem(p2 + 2, y2 + 2 * PAD, z2),
            vmem(p2 + 2, y2 + 2 * PAD, z2),
            vmem(p2 + 2, y2 + 2 * PAD, z2),
            vmem(8, LANES),
            vmem(count, 8, LANES),
            vmem(p2, z2 // LANES, y2, LANES),
            vmem(p3 + 2, y3 + 2 * PAD, z3p),
            vmem(p3 + 2, y3 + 2 * PAD, z3p),
            vmem(p3 + 2, y3 + 2 * PAD, z3p),
            vmem(p3 + 2, y3 + 2 * PAD, z3p),
            pltpu.SemaphoreType.DMA((2,)),
            pltpu.SemaphoreType.REGULAR((rounds,)),
            pltpu.SemaphoreType.DMA((4, 2, messages)),
            pltpu.SemaphoreType.DMA((2, count)),
        ],
        compiler_params=pltpu.CompilerParams(
            collective_id=0, has_side_effects=True, vmem_limit_bytes=48 * 1024 * 1024
        ),
    )(right_side, start)


def solution(mesh):
    sizes = (mesh.shape["gx"], mesh.shape["gy"], mesh.shape["gz"])
    spec = P("gx", "gy", "gz")
    return jax.shard_map(
        functools.partial(local, sizes), mesh=mesh, in_specs=(spec, spec), out_specs=spec, check_vma=False
    )
```

time: 55.6 us -> 33.2 us (0.60); the launches traced: 54.7 us -> 33.1 us
  Pallas kernels: 53 us -> 30.5 us
  local copies, waits for them, and re-layouts: 1.67 us -> 2.6 us
    pallas_call x1, Pallas kernels: 53 us -> 30.5 us  [local(): pl.pallas_call(functools.partial(kernel, sizes), out_shape=jax.ShapeDtype...]
    unnamed x1 -> x5, local copies, waits for them, and re-layouts: 1.67 us -> 2.6 us
where the time goes in v1:
time: 33.2 us; the launch traced here: 33.1 us
  Pallas kernels  30.5 us (92%)
  local copies, waits for them, and re-layouts  2.6 us (8%)
    pallas_call x1, Pallas kernels, local(): pl.pallas_call(functools.partial(kernel, sizes), out_shape=jax.ShapeDtype...  30.5 us
    unnamed x5, local copies, waits for them, and re-layouts  2.6 us

profile of v1, /device:TPU:0, one launch (start us, length us, event | category | flops | bytes accessed | tf_op | source)
XLA Modules:
  0.0 33.1 jit_solution(7081514147358175752)
XLA Ops:
  0.0 0.0 copy-start
  0.0 0.9 %copy-done = f32[8,64,128]{2,1,0:T(8,128)S(1)} copy-done((f32[8,64,128]{2,1,0:T(8,128)S(1)}, f32[8,64,128]{2,1,0:T(8,128)}, u32[]{:S(2)}) %copy-start) | copy-done | bytes 262168
  1.0 0.0 copy-start.1
  1.0 0.9 %copy-done.1 = f32[8,64,128]{2,1,0:T(8,128)S(1)} copy-done((f32[8,64,128]{2,1,0:T(8,128)S(1)}, f32[8,64,128]{2,1,0:T(8,128)}, u32[]{:S(2)}) %copy-start.1) | copy-done | bytes 262168
  1.9 30.5 %shard_map.28 = f32[8,64,128]{2,1,0:T(8,128)S(1)} custom-call(f32[8,64,128]{2,1,0:T(8,128)S(1)} %copy-done, f32[8,64,128]{2,1,0:T(8,128)S(1)} %copy-done.1), custom_call_target="tpu_custom_call" | custom-call | tf_op jit(solution)/shard_map/pallas_call | solution.py:897
  32.4 0.7 %copy.4 = f32[8,64,128]{2,1,0:T(8,128)} copy(f32[8,64,128]{2,1,0:T(8,128)S(1)} %shard_map.28) | data formatting | bytes 524288
Async XLA Ops:
  0.0 0.9 %copy-start = (f32[8,64,128]{2,1,0:T(8,128)S(1)}, f32[8,64,128]{2,1,0:T(8,128)}, u32[]{:S(2)}) copy-start(f32[8,64,128]{2,1,0:T(8,128)} %rhs_hbm.1) | copy-start | bytes 786436
  1.0 0.9 %copy-start.1 = (f32[8,64,128]{2,1,0:T(8,128)S(1)}, f32[8,64,128]{2,1,0:T(8,128)}, u32[]{:S(2)}) copy-start(f32[8,64,128]{2,1,0:T(8,128)} %start_hbm.1) | copy-start | bytes 786436

commit v2 on v1

--- a/solution.py
+++ b/solution.py
@@ -20,6 +20,7 @@
 RHS1 = 5
 COR1 = 6
 COR0 = 4
+GRANT = 56150000
 
 
 def dot(a, b):
@@ -96,7 +97,7 @@
     def __init__(self, sems):
         self.sems, self.count, self.items = sems, 0, []
 
-    def add(self, src, dst, send, recv, peer):
+    def add(self, src, dst, send, recv, peer, tag=None):
         at = self.count
         self.count += 1
         copy = pltpu.make_async_remote_copy(
@@ -107,18 +108,21 @@
             device_id=peer,
             device_id_type=MESH,
         )
-        self.items.append((copy, send, recv))
+        self.items.append((tag, copy, send, recv))
         when(send, copy.start)
 
-    def wait(self):
-        for copy, send, recv in self.items:
-            when(send, copy.wait_send)
-            when(recv, copy.wait_recv)
+    def wait(self, tag=None):
+        for item in list(self.items):
+            name, copy, send, recv = item
+            if tag is None or name == tag:
+                when(send, copy.wait_send)
+                when(recv, copy.wait_recv)
+                self.items.remove(item)
 
 
 def kernel(
     sizes, rhs_hbm, start_hbm, out_ref,
-    rhs, start, a0, r0, f0, s0, merged_out, merged_in, zsend, zrecv, esend, erecv,
+    rhs, start, a0, r0, f0, s0, merged_out, merged_in, zsend, zrecv, esend, erecv, yedge_out, yedge_in,
     a1, r1, b1, f1, s1, w0, w1, tiles_out, tiles_in, ysides, xysides, zout, zin,
     n_out, n_in, ny_in, nxy_in, nz_out, nz_in, g_out, g_in,
     b2r, b2b, r2, v2, pack, slots, w2, b3r, b3b, r3, v3,
@@ -181,7 +185,7 @@
 
     heard = sum([(1 if recv is True else jnp.where(recv, 1, 0)) for _, recv, _ in faces])
 
-    for ref in (zrecv, erecv, merged_in):
+    for ref in (zrecv, erecv, merged_in, yedge_in):
         ref[...] = jnp.zeros_like(ref)
     rows0 = a0.shape[3]
     for q in range(3):
@@ -260,7 +264,7 @@
             packed = jnp.where(here, turn(v, FACE * t - first), packed)
         zsend[zi] = packed
     for zi, d in enumerate(zdirs):
-        mail.add(zsend.at[zi], zrecv.at[zi, pl.ds(8, ly)], *to(None, 0, d))
+        mail.add(zsend.at[zi], zrecv.at[zi, pl.ds(8, ly)], *to(None, 0, d), "z")
 
     width = sum(w for _, _, w in EDGE)
     starts = [sum(w for _, _, w in EDGE[:t]) for t in range(len(EDGE))]
@@ -275,40 +279,33 @@
                     here = (lane8 >= lo) & (lane8 < lo + w)
                     packed = jnp.where(here, turn(v[8 * g:8 * g + 8], lo - first), packed)
             esend[s, zi] = packed
+        for yi, d in enumerate(ydirs):
+            for (q, k, w), at in zip(EDGE, starts):
+                first = TOP + ly - w if d > 0 else TOP
+                yedge_out[s, yi, at:at + w] = a0[q, side.outward(c, n0, k), 0, first:first + w]
     pl.semaphore_wait(relay.at[0], heard)
     signal_faces(relay.at[1])
     for s, side in enumerate(near):
-        p_src, p_dst = side.source(c, n0, 2), side.target(c, n0, 2)
-        for d in ydirs:
-            src, dst = strip(d, ly)
-            mail.add(
-                a0.at[0:3, pl.ds(p_src, 2), 0, pl.ds(src, 8)],
-                a0.at[0:3, pl.ds(p_dst, 2), 0, pl.ds(dst, 8)],
-                *to(side, d, 0),
-            )
+        for yi, d in enumerate(ydirs):
+            mail.add(yedge_out.at[s, yi], yedge_in.at[s, yi], *to(side, d, 0), "y")
     for zi, dz in enumerate(zdirs):
         for d in ydirs:
             src, dst = strip(d, ly)
             mail.add(
-                zsend.at[zi, pl.ds(src - TOP, 8)], zrecv.at[zi, pl.ds(dst - 8, 8)], *to(None, d, dz)
+                zsend.at[zi, pl.ds(src - TOP, 8)], zrecv.at[zi, pl.ds(dst - 8, 8)], *to(None, d, dz), "z"
             )
         for s, side in enumerate(near):
-            mail.add(esend.at[s, zi], erecv.at[s, zi, 1], *to(side, 0, dz))
+            mail.add(esend.at[s, zi], erecv.at[s, zi, 1], *to(side, 0, dz), "e")
     rounds = relay.shape[0]
     pl.semaphore_wait(relay.at[1], heard)
     for zi, dz in enumerate(zdirs):
         for s, side in enumerate(near):
             for d in ydirs:
-                mail.add(esend.at[s, zi], erecv.at[s, zi, 0 if d > 0 else 2], *to(side, d, dz))
+                mail.add(esend.at[s, zi], erecv.at[s, zi, 0 if d > 0 else 2], *to(side, d, dz), "e")
     for r in range(2, rounds):
         signal_faces(relay.at[r])
         pl.semaphore_wait(relay.at[r], heard)
-    mail.wait()
-
-    for s, side in enumerate(near):
-        v = merged_in[s]
-        a0[0, side.landing(c, n0, 3), 0, own] = v
-        a0[2, side.landing(c, n0, 2), 0, own] = pltpu.roll(v, ly - 1, axis=0)
+    mail.wait("z")
     rows_h = ly + 16
     lane_h = iota((rows_h, LANES), 1)
     for t, (q, i) in enumerate(slots0):
@@ -317,6 +314,7 @@
         a0[q, c + i, 1, PAD:PAD + rows_h] = jnp.where(
             lane_h >= LANES - FACE, low, jnp.where(lane_h < FACE, high, 0.0)
         )
+    mail.wait("e")
     for s, side in enumerate(near):
         for (q, k, w), at in zip(EDGE, starts):
             pair = side.landing(c, n0, k)
@@ -328,6 +326,18 @@
                 a0[q, pair, 1, PAD + 8 * g:PAD + 8 * g + 8] = jnp.where(
                     lane8 >= LANES - w, low, jnp.where(lane8 < w, high, 0.0)
                 )
+
+    mail.wait("y")
+    for s, side in enumerate(near):
+        for yi, d in enumerate(ydirs):
+            for (q, k, w), at in zip(EDGE, starts):
+                first = TOP - w if d > 0 else TOP + ly
+                a0[q, side.landing(c, n0, k), 0, first:first + w] = yedge_in[s, yi, at:at + w]
+    mail.wait()
+    for s, side in enumerate(near):
+        v = merged_in[s]
+        a0[0, side.landing(c, n0, 3), 0, own] = v
+        a0[2, side.landing(c, n0, 2), 0, own] = pltpu.roll(v, ly - 1, axis=0)
 
     def span(n, k):
         if gx == 1:
@@ -562,19 +572,42 @@
     def number(at):
         return (at[0] * gy + at[1]) * gz + at[2]
 
+    def flipped(at, k):
+        bit = 1
+        while bit <= k:
+            if k & bit:
+                at = at + bit - 2 * bit * lax.rem(lax.div(at, bit), 2)
+            bit *= 2
+        return at
+
+    def partners():
+        own_at = (mx, my, mz)
+        flips = [[flipped(at, k) for k in range(size)] for at, size in zip(own_at, sizes)]
+        order = [(i, j, k) for i in range(gx) for j in range(gy) for k in range(gz)][1:]
+        order.sort(key=lambda f: (-(f[0] + min(f[2], 2) + f[1] // 2), -f[1], f[2]))
+        for f in order:
+            at = tuple(flips[axis][k] for axis, k in enumerate(f))
+            close = True
+            for a, b, k, reach in zip(at, own_at, f, dist):
+                if k > reach:
+                    close = both(close, (a - b <= reach) & (b - a <= reach))
+            yield at, close
+
+    straight = count <= 64 and all(size & (size - 1) == 0 for size in sizes)
+
     def others(body):
-        if count <= 64:
-            for k in range(1, count):
-                body(k)
+        if straight:
+            for place in partners():
+                body(place)
         else:
             def step(k, carry):
-                body(k)
+                body(coords(k))
                 return carry
 
             lax.fori_loop(1, count, step, 0)
 
-    def gather(k, arriving):
-        at, close = coords(k)
+    def gather(place, arriving):
+        at, close = place
         d = number(at)
         return pltpu.make_async_remote_copy(
             src_ref=pack,
@@ -585,12 +618,12 @@
             device_id_type=MESH,
         ), close
 
-    def gather_start(k):
-        copy, close = gather(k, False)
+    def gather_start(place):
+        copy, close = gather(place, False)
         when(close, copy.start)
 
-    def gather_wait(k):
-        copy, close = gather(k, True)
+    def gather_wait(place):
+        copy, close = gather(place, True)
 
         def done():
             copy.wait_send()
@@ -912,6 +945,8 @@
             vmem(2, ly + 16, LANES),
             vmem(near_a, 2, 8, LANES),
             vmem(near_a, 2, 3, 8, LANES),
+            vmem(near_a, 2, 16, LANES),
+            vmem(near_a, 2, 16, LANES),
             vmem(2, m1, 1, r1, LANES),
             vmem(m1, 1, r1, LANES),
             vmem(m1, 1, r1, LANES),
@@ -950,7 +985,7 @@
             pltpu.SemaphoreType.DMA((2, count)),
         ],
         compiler_params=pltpu.CompilerParams(
-            collective_id=0, has_side_effects=True, vmem_limit_bytes=48 * 1024 * 1024
+            collective_id=0, has_side_effects=True, vmem_limit_bytes=GRANT
         ),
     )(right_side, start)
 

time: 33.2 us -> 30.2 us (0.910)
  local copies, waits for them, and re-layouts: 2.6 us -> 0.71 us
  Pallas kernels: 30.5 us -> 29.4 us
    unnamed x5 -> x1, local copies, waits for them, and re-layouts: 2.6 us -> 0.71 us
    pallas_call x1, Pallas kernels: 30.5 us -> 29.4 us  [local(): pl.pallas_call(functools.partial(kernel, sizes), out_shape=jax.ShapeDtype...]
where the time goes in v2:
time: 30.2 us; the launch traced here: 30.1 us
  Pallas kernels  29.4 us (97%)
  local copies, waits for them, and re-layouts  0.71 us (2%)
    pallas_call x1, Pallas kernels, local(): pl.pallas_call(functools.partial(kernel, sizes), out_shape=jax.ShapeDtype...  29.4 us
    unnamed x1, local copies, waits for them, and re-layouts  0.71 us

profile of v2, /device:TPU:0, one launch (start us, length us, event | category | flops | bytes accessed | tf_op | source)
XLA Modules:
  0.0 30.1 jit_solution(5851779244212676047)
XLA Ops:
  0.0 29.4 %shard_map.28 = f32[8,64,128]{2,1,0:T(8,128)S(1)} custom-call(f32[8,64,128]{2,1,0:T(8,128)} %rhs_hbm.1, f32[8,64,128]{2,1,0:T(8,128)} %start_hbm.1), custom_call_target="tpu_custom_call" | custom-call | tf_op jit(solution)/shard_map/pallas_call | solution.py:930
  29.4 0.7 %copy.4 = f32[8,64,128]{2,1,0:T(8,128)} copy(f32[8,64,128]{2,1,0:T(8,128)S(1)} %shard_map.28) | data formatting | bytes 524288

commit v3 on v2

--- a/solution.py
+++ b/solution.py
@@ -24,7 +24,16 @@
 
 
 def dot(a, b):
-    return jnp.dot(a, b, precision=lax.Precision.HIGHEST, preferred_element_type=jnp.float32)
+    high = a.astype(jnp.bfloat16)
+    rest = a - high.astype(jnp.float32)
+    middle = rest.astype(jnp.bfloat16)
+    low = (rest - middle.astype(jnp.float32)).astype(jnp.bfloat16)
+    b = b.astype(jnp.bfloat16)
+    return jnp.dot(
+        jnp.concatenate([high, middle, low], axis=1),
+        jnp.concatenate([b, b, b], axis=0),
+        preferred_element_type=jnp.float32,
+    )
 
 
 def iota(shape, axis):
@@ -185,26 +194,26 @@
 
     heard = sum([(1 if recv is True else jnp.where(recv, 1, 0)) for _, recv, _ in faces])
 
-    for ref in (zrecv, erecv, merged_in, yedge_in):
-        ref[...] = jnp.zeros_like(ref)
+    def clear(*refs):
+        for ref in refs:
+            ref[...] = jnp.zeros_like(ref)
+
     rows0 = a0.shape[3]
+    own = slice(TOP, TOP + ly)
+    outside = [i for i in range(a0.shape[1]) if i < c or i >= c + n0]
+    clear(zrecv, erecv, yedge_in)
     for q in range(3):
-        for i in range(a0.shape[1]):
-            if i < c or i >= c + n0:
-                a0[q, i, 0] = jnp.zeros((rows0, LANES), jnp.float32)
-            else:
-                a0[q, i, 0, 0:TOP] = jnp.zeros((TOP, LANES), jnp.float32)
-                a0[q, i, 0, TOP + ly:] = jnp.zeros((rows0 - TOP - ly, LANES), jnp.float32)
+        for i in range(c, c + n0):
+            a0[q, i, 0, PAD:TOP] = jnp.zeros((PAD, LANES), jnp.float32)
+            a0[q, i, 0, TOP + ly:TOP + ly + PAD] = jnp.zeros((PAD, LANES), jnp.float32)
+        if gx != 2:
+            for i in outside:
+                a0[q, i, 0, own] = jnp.zeros((ly, LANES), jnp.float32)
+    if gx != 2:
+        clear(merged_in)
     barrier = pltpu.get_barrier_semaphore()
     signal_faces(barrier)
-
-    for ref in (ysides, xysides, tiles_in, zin, n_in, ny_in, nxy_in, nz_in, g_in, slots):
-        ref[...] = jnp.zeros_like(ref)
-    for q in range(3):
-        for i in range(a0.shape[1]):
-            a0[q, i, 1] = jnp.zeros((rows0, LANES), jnp.float32)
-    for ref in (r0, f0):
-        ref[...] = jnp.zeros_like(ref)
+    clear(slots)
 
     def mask(shape, row0, lane_of, bounds):
         y = iota(shape, 0) + row0
@@ -212,12 +221,6 @@
         inside = (y >= 0) & (y < bounds[0]) & (z >= 0) & (z < bounds[1])
         return jnp.where(inside, SIXTH, 0.0)
 
-    fine = (gy * ly, gz * lz)
-    s0[0] = mask(s0.shape[1:], my * ly - PAD, lambda k: mz * lz + k, fine)
-    s0[1] = mask(s0.shape[1:], my * ly - PAD, lambda k: mz * lz + jnp.where(k < 64, k + lz, k - LANES), fine)
-    s1[0] = mask(s1.shape[1:], my * hy - PAD, lambda k: mz * hz + k - left, (gy * hy, gz * hz))
-
-    own = slice(TOP, TOP + ly)
     even = evens(ly, LANES)
     for copy in copies:
         copy.wait()
@@ -240,9 +243,6 @@
         where = to(side, 0, 0)
         src, dst = side.source(c, n0, 2), side.target(c, n0, 2)
         mail.add(a0.at[0:2, pl.ds(src, 2), 0, own], a0.at[0:2, pl.ds(dst, 2), 0, own], *where)
-        src, dst = side.source(c, n0, 1), side.target(c, n0, 1)
-        mail.add(a0.at[2, pl.ds(src, 1), 0, own], a0.at[2, pl.ds(dst, 1), 0, own], *where)
-        mail.add(merged_out.at[s], merged_in.at[s], *where)
 
     def strip(d, rows):
         return (TOP + rows - 8, TOP - 8) if d > 0 else (TOP, TOP + rows)
@@ -250,9 +250,12 @@
     for d in ydirs:
         src, dst = strip(d, ly)
         mail.add(
-            a0.at[0:3, pl.ds(c, n0), 0, pl.ds(src, 8)], a0.at[0:3, pl.ds(c, n0), 0, pl.ds(dst, 8)], *to(None, d, 0)
+            a0.at[0:3, pl.ds(c, n0), 0, pl.ds(src, 8)],
+            a0.at[0:3, pl.ds(c, n0), 0, pl.ds(dst, 8)],
+            *to(None, d, 0), "z",
         )
     signal_faces(relay.at[0])
+    clear(ysides, xysides, tiles_in, zin, n_in, ny_in, nxy_in, nz_in, g_in)
 
     slots0 = [(q, i) for i in range(n0) for q in range(3)]
     for zi, d in enumerate(zdirs):
@@ -301,10 +304,31 @@
     for zi, dz in enumerate(zdirs):
         for s, side in enumerate(near):
             for d in ydirs:
-                mail.add(esend.at[s, zi], erecv.at[s, zi, 0 if d > 0 else 2], *to(side, d, dz), "e")
+                half = pl.ds(4 if d > 0 else 0, 4)
+                mail.add(esend.at[s, zi, half], erecv.at[s, zi, 0 if d > 0 else 2, half], *to(side, d, dz), "e")
+    for s, side in enumerate(near):
+        where = to(side, 0, 0)
+        src, dst = side.source(c, n0, 1), side.target(c, n0, 1)
+        mail.add(a0.at[2, pl.ds(src, 1), 0, own], a0.at[2, pl.ds(dst, 1), 0, own], *where)
+        mail.add(merged_out.at[s], merged_in.at[s], *where)
     for r in range(2, rounds):
         signal_faces(relay.at[r])
         pl.semaphore_wait(relay.at[r], heard)
+    clear(r0, f0)
+    for q in range(3):
+        for i in range(a0.shape[1]):
+            a0[q, i, 1] = jnp.zeros((rows0, LANES), jnp.float32)
+            edge = PAD if c <= i < c + n0 else TOP
+            a0[q, i, 0, 0:edge] = jnp.zeros((edge, LANES), jnp.float32)
+            a0[q, i, 0, rows0 - edge:] = jnp.zeros((edge, LANES), jnp.float32)
+    if gx == 2:
+        for k in range(1, HALO + 1):
+            a0[0, jnp.where(mx == 0, c - k, c + n0 + k - 1), 0, own] = jnp.zeros((ly, LANES), jnp.float32)
+    fine = (gy * ly, gz * lz)
+    s0[0] = mask(s0.shape[1:], my * ly - PAD, lambda k: mz * lz + k, fine)
+    s0[1] = mask(s0.shape[1:], my * ly - PAD, lambda k: mz * lz + jnp.where(k < 64, k + lz, k - LANES), fine)
+    s1[0] = mask(s1.shape[1:], my * hy - PAD, lambda k: mz * hz + k - left, (gy * hy, gz * hz))
+
     mail.wait("z")
     rows_h = ly + 16
     lane_h = iota((rows_h, LANES), 1)
@@ -314,31 +338,6 @@
         a0[q, c + i, 1, PAD:PAD + rows_h] = jnp.where(
             lane_h >= LANES - FACE, low, jnp.where(lane_h < FACE, high, 0.0)
         )
-    mail.wait("e")
-    for s, side in enumerate(near):
-        for (q, k, w), at in zip(EDGE, starts):
-            pair = side.landing(c, n0, k)
-            for g in range(groups0 + 2):
-                which, group = (0, groups0 - 1) if g == 0 else ((2, 0) if g > groups0 else (1, g - 1))
-                lo = width * group + at
-                low = turn(erecv[s, 0, which], LANES - w - lo)
-                high = turn(erecv[s, 1, which], -lo)
-                a0[q, pair, 1, PAD + 8 * g:PAD + 8 * g + 8] = jnp.where(
-                    lane8 >= LANES - w, low, jnp.where(lane8 < w, high, 0.0)
-                )
-
-    mail.wait("y")
-    for s, side in enumerate(near):
-        for yi, d in enumerate(ydirs):
-            for (q, k, w), at in zip(EDGE, starts):
-                first = TOP - w if d > 0 else TOP + ly
-                a0[q, side.landing(c, n0, k), 0, first:first + w] = yedge_in[s, yi, at:at + w]
-    mail.wait()
-    for s, side in enumerate(near):
-        v = merged_in[s]
-        a0[0, side.landing(c, n0, 3), 0, own] = v
-        a0[2, side.landing(c, n0, 2), 0, own] = pltpu.roll(v, ly - 1, axis=0)
-
     def span(n, k):
         if gx == 1:
             return c, n
@@ -368,8 +367,8 @@
             out.append(total + (low[g] + high[g]))
         return out
 
-    def relax(dst, src, rhs_of, scale, n, k, red, factor, tiles=None, emit=None):
-        first, length = span(n, k)
+    def relax(dst, src, rhs_of, scale, n, k, red, factor, tiles=None, emit=None, part=None):
+        first, length = part or span(n, k)
         held = src.shape[1]
         rows = src.shape[2]
         lo, hi = (TOP, rows - TOP) if emit else (PAD, rows - PAD)
@@ -410,12 +409,48 @@
 
     black0 = a0.at[0]
     rhs0 = [lambda i, g, lo, hi, q=q: a0[q, i, g, lo:hi] for q in (1, 2)]
+    def sweep0(step, part):
+        if step % 2 == 0:
+            relax(r0, black0, rhs0[0], s0, n0, 0, True, 1.0, part=part)
+        else:
+            relax(black0, r0, rhs0[1], s0, n0, 0, False, 1.0, part=part)
+
+    def early(step):
+        return n0 - 1 - step if gx == 2 else 0
+
     for step in range(4):
-        k = (4 - step + 1) // 2
-        if step % 2 == 0:
-            relax(r0, black0, rhs0[0], s0, n0, k, True, 1.0)
-        else:
-            relax(black0, r0, rhs0[1], s0, n0, k, False, 1.0)
+        if early(step) > 0:
+            sweep0(step, (jnp.where(mx == 0, c, c + n0 - early(step)), early(step)))
+    mail.wait("e")
+    for s, side in enumerate(near):
+        for (q, k, w), at in zip(EDGE, starts):
+            pair = side.landing(c, n0, k)
+            for g in range(groups0 + 2):
+                which, group = (0, groups0 - 1) if g == 0 else ((2, 0) if g > groups0 else (1, g - 1))
+                lo = width * group + at
+                low = turn(erecv[s, 0, which], LANES - w - lo)
+                high = turn(erecv[s, 1, which], -lo)
+                a0[q, pair, 1, PAD + 8 * g:PAD + 8 * g + 8] = jnp.where(
+                    lane8 >= LANES - w, low, jnp.where(lane8 < w, high, 0.0)
+                )
+
+    mail.wait("y")
+    for s, side in enumerate(near):
+        for yi, d in enumerate(ydirs):
+            for (q, k, w), at in zip(EDGE, starts):
+                first = TOP - w if d > 0 else TOP + ly
+                a0[q, side.landing(c, n0, k), 0, first:first + w] = yedge_in[s, yi, at:at + w]
+    mail.wait()
+    for s, side in enumerate(near):
+        v = merged_in[s]
+        a0[0, side.landing(c, n0, 3), 0, own] = v
+        a0[2, side.landing(c, n0, 2), 0, own] = pltpu.roll(v, ly - 1, axis=0)
+    for step in range(4):
+        first, length = span(n0, (4 - step + 1) // 2)
+        done = max(early(step), 0)
+        if done:
+            first = first + jnp.where(mx == 0, done, 0)
+        sweep0(step, (first, length - done))
     for j in range(n0):
         w0[j * ly:(j + 1) * ly, :] = residual(r0, black0, rhs0[0], rhs0[1], n0, j, 1.0)
     r = w0[pl.ds(0, n0 * hy, stride=2), :] + w0[pl.ds(1, n0 * hy, stride=2), :]

time: 30.2 us -> 29.5 us (0.977)
  Pallas kernels: 29.4 us -> 28.6 us
    pallas_call x1, Pallas kernels: 29.4 us -> 28.6 us  [local(): pl.pallas_call(functools.partial(kernel, sizes), out_shape=jax.ShapeDtype...]
where the time goes in v3:
time: 29.5 us; the launch traced here: 29.3 us
  Pallas kernels  28.6 us (97%)
  local copies, waits for them, and re-layouts  0.71 us (2%)
    pallas_call x1, Pallas kernels, local(): pl.pallas_call(functools.partial(kernel, sizes), out_shape=jax.ShapeDtype...  28.6 us
    unnamed x1, local copies, waits for them, and re-layouts  0.71 us

profile of v3, /device:TPU:0, one launch (start us, length us, event | category | flops | bytes accessed | tf_op | source)
XLA Modules:
  0.0 29.3 jit_solution(4171803230625274854)
XLA Ops:
  0.0 28.6 %shard_map.28 = f32[8,64,128]{2,1,0:T(8,128)S(1)} custom-call(f32[8,64,128]{2,1,0:T(8,128)} %rhs_hbm.1, f32[8,64,128]{2,1,0:T(8,128)} %start_hbm.1), custom_call_target="tpu_custom_call" | custom-call | tf_op jit(solution)/shard_map/pallas_call | solution.py:965
  28.6 0.7 %copy.4 = f32[8,64,128]{2,1,0:T(8,128)} copy(f32[8,64,128]{2,1,0:T(8,128)S(1)} %shard_map.28) | data formatting | bytes 524288

commit v4 on v3

--- a/solution.py
+++ b/solution.py
@@ -743,12 +743,47 @@
             _, total = coarse_total(src, i, red, rows, full)
             dst[i, PAD:PAD + rows] = (b[i, PAD:PAD + rows] * factor + total) * scale
 
+    def sweep(red, black, red_rhs, black_rhs, pairs, factor, rows, scale, full):
+        width_z = black.shape[2]
+        lo, hi = PAD, PAD + rows
+        lane = iota((rows, width_z), 1)
+        chess = evens(rows, width_z)
+
+        def moved(v, k):
+            out = turn(v, k)
+            if full:
+                out = jnp.where(lane < k, 0.0, out) if k > 0 else jnp.where(lane >= width_z + k, 0.0, out)
+            return out
+
+        here, before, after = scale
+        beside_z = []
+        for i in range(1, pairs + 1):
+            v = black[i, lo:hi]
+            beside = jnp.where(chess, black[i - 1, lo:hi], black[i + 1, lo:hi])
+            rest = (red_rhs[i, lo:hi] * factor + (v + beside)) + (black[i, lo - 1:hi - 1] + black[i, lo + 1:hi + 1])
+            red[i, lo:hi] = (rest + (moved(v, 1) + moved(v, -1))) * here
+            low = (turn(rest, 1) + (moved(v, 2) + v)) * before
+            high = (turn(rest, -1) + (v + moved(v, -2))) * after
+            beside_z.append(low + high)
+        for i in range(1, pairs + 1):
+            v = red[i, lo:hi]
+            beside = jnp.where(chess, red[i + 1, lo:hi], red[i - 1, lo:hi])
+            total = (v + beside) + (red[i, lo - 1:hi - 1] + red[i, lo + 1:hi + 1])
+            black[i, lo:hi] = (black_rhs[i, lo:hi] * factor + (total + beside_z[i - 1])) * here
+
+    def scales(rows, width_z, cells):
+        lane = iota((rows, width_z), 1)
+        return tuple(
+            jnp.where((lane - k >= 0) & (lane - k < cells), SIXTH, 0.0) if k or cells < width_z else SIXTH
+            for k in (0, 1, -1)
+        )
+
     in2 = slice(PAD, PAD + y2)
+    scale2 = scales(y2, z2, z2)
     for i in range(1, p2 + 1):
         r2[i, in2] = (b2r[i, in2] * 16.0) * SIXTH
     coarse(v2, r2, b2b, p2, False, 16.0, y2, SIXTH, True)
-    coarse(r2, v2, b2r, p2, True, 16.0, y2, SIXTH, True)
-    coarse(v2, r2, b2b, p2, False, 16.0, y2, SIXTH, True)
+    sweep(r2, v2, b2r, b2b, p2, 16.0, y2, scale2, True)
 
     fold = jnp.where(iota((z2, z3p), 1) == iota((z2, z3p), 0) // 2, 0.125, 0.0)
     parts = []
@@ -777,11 +812,10 @@
         b3b[1 + j, in3] = jnp.where(chess3, two, one)
 
     full3 = z3 == z3p
-    scale3 = SIXTH if full3 else jnp.where(iota((y3, z3p), 1) < z3, SIXTH, 0.0)
+    scale3 = scales(y3, z3p, z3)
 
     def sweep3(_, carry):
-        coarse(r3, v3, b3r, p3, True, 64.0, y3, scale3, full3)
-        coarse(v3, r3, b3b, p3, False, 64.0, y3, scale3, full3)
+        sweep(r3, v3, b3r, b3b, p3, 64.0, y3, scale3, full3)
         return carry
 
     if p3 == 1:
@@ -808,8 +842,7 @@
             lanes = slice(LANES * g, LANES * (g + 1))
             v2[1 + i, in2, lanes] = v2[1 + i, in2, lanes] + w2[i, g, 0:y2]
     for _ in range(2):
-        coarse(r2, v2, b2r, p2, True, 16.0, y2, SIXTH, True)
-        coarse(v2, r2, b2b, p2, False, 16.0, y2, SIXTH, True)
+        sweep(r2, v2, b2r, b2b, p2, 16.0, y2, scale2, True)
 
     mail1.wait()
     grow1 = jnp.where(

time: 29.5 us -> 29.1 us (0.986)
  Pallas kernels: 28.6 us -> 28.2 us
    pallas_call x1, Pallas kernels: 28.6 us -> 28.2 us  [local(): pl.pallas_call(functools.partial(kernel, sizes), out_shape=jax.ShapeDtype...]
where the time goes in v4:
time: 29.1 us; the launch traced here: 28.9 us
  Pallas kernels  28.2 us (97%)
  local copies, waits for them, and re-layouts  0.71 us (2%)
    pallas_call x1, Pallas kernels, local(): pl.pallas_call(functools.partial(kernel, sizes), out_shape=jax.ShapeDtype...  28.2 us
    unnamed x1, local copies, waits for them, and re-layouts  0.71 us

profile of v4, /device:TPU:0, one launch (start us, length us, event | category | flops | bytes accessed | tf_op | source)
XLA Modules:
  0.0 28.9 jit_solution(16911326862864994944)
XLA Ops:
  0.0 28.2 %shard_map.28 = f32[8,64,128]{2,1,0:T(8,128)S(1)} custom-call(f32[8,64,128]{2,1,0:T(8,128)} %rhs_hbm.1, f32[8,64,128]{2,1,0:T(8,128)} %start_hbm.1), custom_call_target="tpu_custom_call" | custom-call | tf_op jit(solution)/shard_map/pallas_call | solution.py:998
  28.2 0.7 %copy.4 = f32[8,64,128]{2,1,0:T(8,128)} copy(f32[8,64,128]{2,1,0:T(8,128)S(1)} %shard_map.28) | data formatting | bytes 524288

commit v5 on v4

--- a/solution.py
+++ b/solution.py
@@ -479,20 +479,24 @@
                 packed = jnp.where(here, turn(read(t), w * t - first), packed)
             yield packed
 
-    def post1(mail, out, into, y_in, xy_in, z_out, z_in):
+    def post1(mail, out, into, y_in, xy_in, z_out, z_in, corner):
+        far_first = list(enumerate([None] + sides1))[::-1]
+        for steps in ((1, -1), (0,)):
+            for s, side in far_first:
+                for zi, dz in enumerate(zdirs):
+                    for d in steps:
+                        few = corner if d and side is not None else 8
+                        rows = pl.ds(8 - few if d > 0 else 0, few)
+                        mail.add(z_out.at[zi, rows], z_in.at[zi, s, 1 - d, rows], *to(side, d, dz))
+        for s, side in enumerate(sides1):
+            for yi, d in enumerate(ydirs):
+                src = hy - 8 if d > 0 else 0
+                mail.add(out.at[:, pl.ds(src, 8)], xy_in.at[s, yi], *to(side, d, 0))
         for s, side in enumerate(sides1):
             mail.add(out, into.at[s], *to(side, 0, 0))
         for yi, d in enumerate(ydirs):
             src = hy - 8 if d > 0 else 0
             mail.add(out.at[:, pl.ds(src, 8)], y_in.at[yi], *to(None, d, 0))
-        for s, side in enumerate(sides1):
-            for yi, d in enumerate(ydirs):
-                src = hy - 8 if d > 0 else 0
-                mail.add(out.at[:, pl.ds(src, 8)], xy_in.at[s, yi], *to(side, d, 0))
-        for zi, dz in enumerate(zdirs):
-            for s, side in enumerate([None] + sides1):
-                for yi, d in enumerate((1, 0, -1)):
-                    mail.add(z_out.at[zi], z_in.at[zi, s, yi], *to(side, d, dz))
 
     def regions1():
         yield from ((None, None, j, c + j) for j in range(n1))
@@ -523,7 +527,7 @@
     for zi, packed in enumerate(pack_edges(tile_of, items, RHS1)):
         zout[zi] = packed
     mail = Mail(sems.at[1])
-    post1(mail, tiles_out, tiles_in, ysides, xysides, zout, zin)
+    post1(mail, tiles_out, tiles_in, ysides, xysides, zout, zin, 4)
     for ref in (a1, r1, b1, f1):
         for i in range(ref.shape[-4]):
             halo_pair = i < c or i >= c + n1
@@ -619,7 +623,7 @@
         own_at = (mx, my, mz)
         flips = [[flipped(at, k) for k in range(size)] for at, size in zip(own_at, sizes)]
         order = [(i, j, k) for i in range(gx) for j in range(gy) for k in range(gz)][1:]
-        order.sort(key=lambda f: (-(f[0] + min(f[2], 2) + f[1] // 2), -f[1], f[2]))
+        order.sort(key=lambda f: (-f[0], -min(f[2], 2), -f[1]))
         for f in order:
             at = tuple(flips[axis][k] for axis, k in enumerate(f))
             close = True
@@ -675,7 +679,7 @@
     for zi, packed in enumerate(pack_edges(tile_n, n1, COR1)):
         nz_out[zi] = packed
     mail1 = Mail(sems.at[2])
-    post1(mail1, n_out, n_in, ny_in, nxy_in, nz_out, nz_in)
+    post1(mail1, n_out, n_in, ny_in, nxy_in, nz_out, nz_in, 8)
 
     for zi, d in enumerate(zdirs):
         packed = jnp.zeros((8, LANES), jnp.float32)

time: 29.1 us -> 28.5 us (0.979)
  Pallas kernels: 28.2 us -> 27.6 us
    pallas_call x1, Pallas kernels: 28.2 us -> 27.6 us  [local(): pl.pallas_call(functools.partial(kernel, sizes), out_shape=jax.ShapeDtype...]
where the time goes in v5:
time: 28.5 us; the launch traced here: 28.3 us
  Pallas kernels  27.6 us (97%)
  local copies, waits for them, and re-layouts  0.71 us (2%)
    pallas_call x1, Pallas kernels, local(): pl.pallas_call(functools.partial(kernel, sizes), out_shape=jax.ShapeDtype...  27.6 us
    unnamed x1, local copies, waits for them, and re-layouts  0.71 us

profile of v5, /device:TPU:0, one launch (start us, length us, event | category | flops | bytes accessed | tf_op | source)
XLA Modules:
  0.0 28.3 jit_solution(5960466877253776495)
XLA Ops:
  0.0 27.6 %shard_map.28 = f32[8,64,128]{2,1,0:T(8,128)S(1)} custom-call(f32[8,64,128]{2,1,0:T(8,128)} %rhs_hbm.1, f32[8,64,128]{2,1,0:T(8,128)} %start_hbm.1), custom_call_target="tpu_custom_call" | custom-call | tf_op jit(solution)/shard_map/pallas_call | solution.py:1002
  27.6 0.7 %copy.4 = f32[8,64,128]{2,1,0:T(8,128)} copy(f32[8,64,128]{2,1,0:T(8,128)S(1)} %shard_map.28) | data formatting | bytes 524288

commit v6 on v5

--- a/solution.py
+++ b/solution.py
@@ -242,7 +242,7 @@
     for s, side in enumerate(near):
         where = to(side, 0, 0)
         src, dst = side.source(c, n0, 2), side.target(c, n0, 2)
-        mail.add(a0.at[0:2, pl.ds(src, 2), 0, own], a0.at[0:2, pl.ds(dst, 2), 0, own], *where)
+        mail.add(a0.at[0:2, pl.ds(src, 2), 0, own], a0.at[0:2, pl.ds(dst, 2), 0, own], *where, "x")
 
     def strip(d, rows):
         return (TOP + rows - 8, TOP - 8) if d > 0 else (TOP, TOP + rows)
@@ -290,7 +290,8 @@
     signal_faces(relay.at[1])
     for s, side in enumerate(near):
         for yi, d in enumerate(ydirs):
-            mail.add(yedge_out.at[s, yi], yedge_in.at[s, yi], *to(side, d, 0), "y")
+            filled = pl.ds(0, width)
+            mail.add(yedge_out.at[s, yi, filled], yedge_in.at[s, yi, filled], *to(side, d, 0), "y")
     for zi, dz in enumerate(zdirs):
         for d in ydirs:
             src, dst = strip(d, ly)
@@ -416,7 +417,7 @@
             relax(black0, r0, rhs0[1], s0, n0, 0, False, 1.0, part=part)
 
     def early(step):
-        return n0 - 1 - step if gx == 2 else 0
+        return n0 - 1 - step if gx == 2 and n0 >= 4 else 0
 
     for step in range(4):
         if early(step) > 0:
@@ -440,6 +441,11 @@
             for (q, k, w), at in zip(EDGE, starts):
                 first = TOP - w if d > 0 else TOP + ly
                 a0[q, side.landing(c, n0, k), 0, first:first + w] = yedge_in[s, yi, at:at + w]
+    late = 2 if gx == 2 and n0 >= 4 else 0
+    if late:
+        mail.wait("x")
+        for step in range(4):
+            sweep0(step, (jnp.where(mx == 0, c + early(step), c + n0 - late - early(step)), late))
     mail.wait()
     for s, side in enumerate(near):
         v = merged_in[s]
@@ -447,7 +453,7 @@
         a0[2, side.landing(c, n0, 2), 0, own] = pltpu.roll(v, ly - 1, axis=0)
     for step in range(4):
         first, length = span(n0, (4 - step + 1) // 2)
-        done = max(early(step), 0)
+        done = early(step) + late
         if done:
             first = first + jnp.where(mx == 0, done, 0)
         sweep0(step, (first, length - done))

time: 28.5 us -> 28.2 us (0.989)
  no operation moved by 1% of the time
where the time goes in v6:
time: 28.2 us; the launch traced here: 28.1 us
  Pallas kernels  27.4 us (97%)
  local copies, waits for them, and re-layouts  0.71 us (3%)
    pallas_call x1, Pallas kernels, local(): pl.pallas_call(functools.partial(kernel, sizes), out_shape=jax.ShapeDtype...  27.4 us
    unnamed x1, local copies, waits for them, and re-layouts  0.71 us

profile of v6, /device:TPU:0, one launch (start us, length us, event | category | flops | bytes accessed | tf_op | source)
XLA Modules:
  0.0 28.1 jit_solution(13542954858652985111)
XLA Ops:
  0.0 27.4 %shard_map.28 = f32[8,64,128]{2,1,0:T(8,128)S(1)} custom-call(f32[8,64,128]{2,1,0:T(8,128)} %rhs_hbm.1, f32[8,64,128]{2,1,0:T(8,128)} %start_hbm.1), custom_call_target="tpu_custom_call" | custom-call | tf_op jit(solution)/shard_map/pallas_call | solution.py:1008
  27.4 0.7 %copy.4 = f32[8,64,128]{2,1,0:T(8,128)} copy(f32[8,64,128]{2,1,0:T(8,128)S(1)} %shard_map.28) | data formatting | bytes 524288

commit v7 on v6

--- a/solution.py
+++ b/solution.py
@@ -698,14 +698,6 @@
                 packed = jnp.where(here, turn(v[8 * g:8 * g + 8], lo - first), packed)
         g_out[zi] = packed
     mail0 = Mail(sems.at[3])
-    for side in near:
-        src, dst = side.source(c, n0, 2), side.target(c, n0, 2)
-        mail0.add(black0.at[pl.ds(src, 2), 0, own], f0.at[pl.ds(dst, 2), 0, own], *to(side, 0, 0))
-        for d in ydirs:
-            ysrc, ydst = strip(d, ly)
-            mail0.add(
-                black0.at[pl.ds(src, 2), 0, pl.ds(ysrc, 8)], f0.at[pl.ds(dst, 2), 0, pl.ds(ydst, 8)], *to(side, d, 0)
-            )
     for d in ydirs:
         ysrc, ydst = strip(d, ly)
         mail0.add(
@@ -715,6 +707,14 @@
         for s, side in enumerate([None] + near):
             for yi, d in enumerate((1, 0, -1)):
                 mail0.add(g_out.at[zi], g_in.at[zi, s, yi], *to(side, d, dz))
+    for side in near:
+        src, dst = side.source(c, n0, 2), side.target(c, n0, 2)
+        mail0.add(black0.at[pl.ds(src, 2), 0, own], f0.at[pl.ds(dst, 2), 0, own], *to(side, 0, 0))
+        for d in ydirs:
+            ysrc, ydst = strip(d, ly)
+            mail0.add(
+                black0.at[pl.ds(src, 2), 0, pl.ds(ysrc, 8)], f0.at[pl.ds(dst, 2), 0, pl.ds(ydst, 8)], *to(side, d, 0)
+            )
 
     others(gather_wait)
 

time: 28.2 us -> 28.2 us (level)
  no operation moved by 1% of the time
where the time goes in v7:
time: 28.2 us; the launch traced here: 28.1 us
  Pallas kernels  27.4 us (97%)
  local copies, waits for them, and re-layouts  0.71 us (3%)
    pallas_call x1, Pallas kernels, local(): pl.pallas_call(functools.partial(kernel, sizes), out_shape=jax.ShapeDtype...  27.4 us
    unnamed x1, local copies, waits for them, and re-layouts  0.71 us

profile of v7, /device:TPU:0, one launch (start us, length us, event | category | flops | bytes accessed | tf_op | source)
XLA Modules:
  0.0 28.1 jit_solution(7472089602264358379)
XLA Ops:
  0.0 27.4 %shard_map.28 = f32[8,64,128]{2,1,0:T(8,128)S(1)} custom-call(f32[8,64,128]{2,1,0:T(8,128)} %rhs_hbm.1, f32[8,64,128]{2,1,0:T(8,128)} %start_hbm.1), custom_call_target="tpu_custom_call" | custom-call | tf_op jit(solution)/shard_map/pallas_call | solution.py:1008
  27.4 0.7 %copy.4 = f32[8,64,128]{2,1,0:T(8,128)} copy(f32[8,64,128]{2,1,0:T(8,128)S(1)} %shard_map.28) | data formatting | bytes 524288
